TPU v7x, 32 devices: a whole 2x2x4 slice. The times are simulated.
32 devices in a mesh: task: 4 (over y, core), param: 8 (over z, x).
Axes of the slice: x: 2, y: 2, z: 4, core: 2. Of those that a mesh axis runs over, the one named last changes fastest.
Arguments:
- params: bfloat16 [16, 512, 4096], P('task', 'param'), may hold values from -6 to 6
- fisher: float32 [16, 512, 4096], P('task', 'param'), may hold values from 3e-06 to 1, as said below
Outputs:
- merged: bfloat16 [512, 4096], P('param')
Inputs may be any that keep to these rules, and one draw needn't show every extreme that they name: `fisher`: every entry is positive; scales differ strongly between tasks and between regions of rows.
All inputs are finite; a program needn't handle non-finite values.
Results may differ from a plain program's by a relative error of at most 0.00045.
Values may be sent and summed in bfloat16 or wider, within the bound.
No kernel may reach another device: no remote copies, remote signals or barrier semaphores. Data moves between devices by JAX's collectives and lax.ppermute only.
A program may use at most 64 MiB of HBM per device.

v0:
```python
import jax
import jax.numpy as jnp
from jax import lax
from jax.sharding import PartitionSpec as P


def combined_all(value, axis, join):
    pieces = jax.tree.map(lambda part: lax.all_gather(part, axis), value)
    head = jax.tree.map(lambda part: part[0], pieces)
    tail = jax.tree.map(lambda part: part[1:], pieces)
    total, _ = lax.scan(lambda total, share: (join(total, share), None), head, tail)
    return total


def joined(first, second):
    return (jnp.maximum(first[0], second[0]), first[1] + second[1])


def local(params, fisher):
    local_peak = jnp.max(fisher, axis=(1, 2))
    local_total = jnp.sum(fisher, axis=(1, 2))
    peak, total = combined_all((local_peak, local_total), "param", joined)
    count = float(fisher.shape[1] * lax.axis_size("param") * fisher.shape[2])
    factor = count * peak / total
    weight = jnp.clip(fisher / peak[:, None, None], 0.002, 0.25) * factor[:, None, None]
    numer = jnp.sum(weight * params.astype(jnp.float32), axis=0)
    denom = jnp.sum(weight, axis=0)
    numer, denom = lax.psum((numer, denom), "task")
    return (numer / denom).astype(jnp.bfloat16)


def solution(mesh):
    in_specs = (P("task", "param", None), P("task", "param", None))
    out_specs = P("param", None)
    return jax.shard_map(local, mesh=mesh, in_specs=in_specs, out_specs=out_specs, check_vma=False)
```

profile of v0, /device:TPU:0, one launch (start us, length us, event | category | flops | bytes accessed | tf_op | source)
XLA Modules:
  0.0 97.8 jit_solution(13709745537521834636)
XLA Ops:
  6.5 0.0 copy-start.1
  6.5 0.0 copy-start
  6.5 0.0 all-reduce.6.cloned.1.call-start
  6.5 2.7 %fusion.5 = (f32[4]{0:T(128)S(1)}, f32[4]{0:T(128)S(1)}) fusion(f32[4,64,4096]{2,1,0:T(8,128)} %param.5), kind=kLoop, calls=%fused_computation.11 | loop fusion | flops 2097144 | bytes 4194336 | tf_op jit(solution)/shard_map/reduce_sum | solution.py:21
  9.3 0.0 copy-done.1
  9.3 0.7 dynamic-slice
  10.7 0.2 dynamic-update-slice.1
  10.9 0.2 dynamic-update-slice
  11.1 23.1 %all-reduce.2 = (f32[32]{0:T(128)S(1)}, f32[32]{0:T(128)S(1)}) all-reduce(f32[32]{0:T(128)S(1)} %dynamic-update-slice, f32[32]{0:T(128)S(1)} %dynamic-update-slice.1), channel_id=2, replica_groups=mesh['task'=4,'param'=8] {'param'}, use_global_device_ids=true, to_apply=%add | all-reduce | flops 64 | bytes 512
  34.2 0.1 slice.18
  34.3 0.1 slice.19
  34.4 0.1 reshape.9
  34.4 0.1 reshape.8
  34.5 0.2 while.12
  34.8 0.0 copy-done
  34.8 4.9 %fusion.4 = (f32[64,4096]{1,0:T(8,128)}, f32[64,4096]{1,0:T(8,128)}) fusion(f32[4]{0:T(128)S(1)} %multiply_divide_fusion, f32[4,64,4096]{2,1,0:T(8,128)} %param.5, f32[4]{0:T(128)S(1)} %get-tuple-element.33, bf16[4,64,4096]{2,1,0:T(8,128)(2,1)S(1)} %copy-done), kind=kLoop, calls=%fused_computation.10 | loop fusion | flops 6815744 | bytes 8388640 | tf_op jit(solution)/shard_map/reduce_sum | solution.py:27
  39.7 0.0 all-reduce.6.cloned.1.call-update
  39.7 48.8 %all-reduce.6.cloned.1.call-done = (f32[64,4096]{1,0:T(8,128)}, f32[64,4096]{1,0:T(8,128)}) async-done(((f32[64,4096]{1,0:T(8,128)}, f32[64,4096]{1,0:T(8,128)}), (f32[64,4096]{1,0:T(8,128)}, f32[64,4096]{1,0:T(8,128)})) %all-reduce.6.cloned.1.call-update) | async-done | bytes 2097168 | tf_op jit(solution)/shard_map/psum | solution.py:28
  88.5 2.5 %divide_convert_fusion = bf16[64,4096]{1,0:T(8,128)(2,1)} fusion(f32[64,4096]{1,0:T(8,128)} %get-tuple-element.51, f32[64,4096]{1,0:T(8,128)} %get-tuple-element.52), kind=kLoop, calls=%fused_computation.8 | loop fusion | flops 524288 | bytes 2621440 | tf_op jit(solution)/shard_map/convert_element_type | solution.py:29
  (10 shorter events, 0.1 us)
Async XLA Ops:
  6.5 2.8 %copy-start.1 = (u32[32]{0:T(128)S(1)}, u32[32]{0:T(128)}, u32[]{:S(2)}) copy-start(u32[32]{0:T(128)} %constant.22) | copy-start | bytes 388
  6.5 28.2 %copy-start = (bf16[4,64,4096]{2,1,0:T(8,128)(2,1)S(1)}, bf16[4,64,4096]{2,1,0:T(8,128)(2,1)}, u32[]{:S(2)}) copy-start(bf16[4,64,4096]{2,1,0:T(8,128)(2,1)} %param.4) | copy-start | bytes 6291460
  6.5 82.0 %all-reduce.6.cloned.1.call-start = ((), (), s32[]{:S(2)}) async-start(), calls=%async_computation | async-start | bytes 4194304 | tf_op jit(solution)/shard_map/psum | solution.py:28
Sparse Core Ops, SparseCore 0:
  39.8 48.6 all-reduce.5
where the time goes:
time: 98 us; the launch traced here: 97.8 us
  waiting for transfers between devices  48.8 us (50%)
  blocking collectives  23.1 us (24%)
  between operations  14.1 us (14%)
  other arithmetic  10.2 us (10%)
  local copies, waits for them, and re-layouts  1.43 us (1%)
    psum x1, waiting for transfers between devices, local(): numer, denom = lax.psum((numer, denom), 'task')  48.8 us
    unnamed x1, blocking collectives  23.1 us
    reduce_sum x1, other arithmetic, local(): denom = jnp.sum(weight, axis=0)  4.9 us
    reduce_sum x1, other arithmetic, local(): local_total = jnp.sum(fisher, axis=(1, 2))  2.75 us
    convert_element_type x1, other arithmetic, local(): return (numer / denom).astype(jnp.bfloat16)  2.48 us
  transfers between devices with their start and end apart: 1, of which 1 were waited for; matrix products, arithmetic and copies ran while one was open for 0% of the time, Pallas kernels for 0%

commit v1 on v0

v1 whole, which is shorter than its diff:
```python
import jax
import jax.numpy as jnp
from jax import lax
from jax.sharding import PartitionSpec as P


def swap(value, axis, bit):
    size = lax.axis_size(axis)
    return lax.ppermute(value, axis, [(i, i ^ bit) for i in range(size)])


def bits_of(axis):
    size = lax.axis_size(axis)
    return [1 << k for k in range(size.bit_length() - 1)]


def param_stats(fisher):
    peak = jnp.max(fisher, axis=(1, 2))
    total = jnp.sum(fisher, axis=(1, 2))
    for bit in bits_of("param"):
        stats = jnp.stack([peak, total])
        other = swap(stats, "param", bit)
        peak = jnp.maximum(peak, other[0])
        total = total + other[1]
    return peak, total


def keep_send(value, axis, bit):
    half = value.shape[1] // 2
    upper = (lax.axis_index(axis) & bit) != 0
    low, high = value[:, :half], value[:, half:]
    return jnp.where(upper, high, low), jnp.where(upper, low, high)


def local(params, fisher):
    peak, total = param_stats(fisher)
    count = float(fisher.shape[1] * lax.axis_size("param") * fisher.shape[2])
    factor = count * peak / total
    weight = jnp.clip(fisher / peak[:, None, None], 0.002, 0.25) * factor[:, None, None]
    numer = jnp.sum(weight * params.astype(jnp.float32), axis=0)
    denom = jnp.sum(weight, axis=0)
    part = jnp.stack([numer, denom])
    bits = bits_of("task")
    for bit in bits:
        keep, send = keep_send(part, "task", bit)
        part = keep + swap(send, "task", bit)
    merged = (part[0] / part[1]).astype(jnp.bfloat16)
    for bit in reversed(bits):
        other = swap(merged, "task", bit)
        upper = (lax.axis_index("task") & bit) != 0
        merged = jnp.where(upper, jnp.concatenate([other, merged]), jnp.concatenate([merged, other]))
    return merged


def solution(mesh):
    in_specs = (P("task", "param", None), P("task", "param", None))
    out_specs = P("param", None)
    return jax.shard_map(local, mesh=mesh, in_specs=in_specs, out_specs=out_specs, check_vma=False)
```

time: 98 us -> 46.1 us (0.47)
  waiting for transfers between devices: 48.8 us -> 24.5 us
  blocking collectives: 23.1 us -> 0 us
  between operations: 14.1 us -> 0.05 us
  starting transfers between devices: 0.01 us -> 12.1 us
  local copies, waits for them, and re-layouts: 1.43 us -> 0 us
    psum x1 -> x0, waiting for transfers between devices: 48.8 us -> none  [local(): numer, denom = lax.psum((numer, denom), 'task')]
    ppermute x0 -> x7, waiting for transfers between devices: none -> 24.5 us  [swap(): return lax.ppermute(value, axis, [(i, i ^ bit) for i in range(size)])]
    unnamed x1 -> x0, blocking collectives: 23.1 us -> none
    ppermute x0 -> x7, starting transfers between devices: none -> 12.1 us  [swap(): return lax.ppermute(value, axis, [(i, i ^ bit) for i in range(size)])]
    reduce_sum x2 -> x1, other arithmetic: 7.65 us -> 4.24 us  [local(): numer = jnp.sum(weight * params.astype(jnp.float32), axis=0)]
    reduce_max x0 -> x1, other arithmetic: none -> 2.6 us  [param_stats(): peak = jnp.max(fisher, axis=(1, 2))]
    convert_element_type x1, other arithmetic: 2.48 us -> 0.04 us  [local(): merged = (part[0] / part[1]).astype(jnp.bfloat16)]
    select_n x0 -> x4, other arithmetic: none -> 2.09 us  [the longest x2 1.16 us: keep_send(): return (jnp.where(upper, high, low), jnp.where(upper, low, high))]
  transfers between devices with their start and end apart: 1 -> 7, of which waited for: 1 -> 7; matrix products, arithmetic and copies ran while one was open for 0% -> 0% of each run, Pallas kernels for 0% -> 0%
where the time goes in v1:
time: 46.1 us; the launch traced here: 45.9 us
  waiting for transfers between devices  24.5 us (53%)
  starting transfers between devices  12.1 us (26%)
  other arithmetic  9.29 us (20%)
    ppermute x7, waiting for transfers between devices, swap(): return lax.ppermute(value, axis, [(i, i ^ bit) for i in range(size)])  24.5 us
    ppermute x7, starting transfers between devices, swap(): return lax.ppermute(value, axis, [(i, i ^ bit) for i in range(size)])  12.1 us
    reduce_sum x1, other arithmetic, local(): numer = jnp.sum(weight * params.astype(jnp.float32), axis=0)  4.24 us
    reduce_max x1, other arithmetic, param_stats(): peak = jnp.max(fisher, axis=(1, 2))  2.6 us
    select_n x2, other arithmetic, keep_send(): return (jnp.where(upper, high, low), jnp.where(upper, low, high))  1.16 us
    select_n x2, other arithmetic, local(): jnp.where(upper, jnp.concatenate([other, merged]), jnp.concatenate([merge...  0.93 us
  transfers between devices with their start and end apart: 7, of which 7 were waited for; matrix products, arithmetic and copies ran while one was open for 0% of the time, Pallas kernels for 0%

profile of v1, /device:TPU:0, one launch (start us, length us, event | category | flops | bytes accessed | tf_op | source)
XLA Modules:
  0.0 45.9 jit_solution(9179621866631995704)
XLA Ops:
  0.0 2.6 %fusion.5 = (f32[4]{0:T(128)S(1)}, f32[4]{0:T(128)S(1)}) fusion(f32[4,64,4096]{2,1,0:T(8,128)} %param.3), kind=kLoop, calls=%fused_computation.30 | loop fusion | flops 2097144 | bytes 4194336 | tf_op jit(solution)/shard_map/reduce_max | solution.py:18
  2.6 3.0 %collective-permute-start = (f32[2,4]{1,0:T(2,128)S(1)}, f32[2,4]{1,0:T(2,128)S(1)}, u32[]{:S(2)}, u32[]{:S(2)}) collective-permute-start(f32[2,4]{1,0:T(2,128)S(1)} %pad_maximum_fusion.1), channel_id=1, source_target_pairs={{0,1},{1,0},{2,3},{3,2},{4,5},{5,4},{6,7},{7,6},{8,9},{9,8},{10,11... | collective-permute-start | bytes 104 | tf_op jit(solution)/shard_map/ppermute | solution.py:9
  5.6 1.6 %collective-permute-done = f32[2,4]{1,0:T(2,128)S(1)} collective-permute-done((f32[2,4]{1,0:T(2,128)S(1)}, f32[2,4]{1,0:T(2,128)S(1)}, u32[]{:S(2)}, u32[]{:S(2)}) %collective-permute-start) | collective-permute-done | bytes 64 | tf_op jit(solution)/shard_map/ppermute | solution.py:9
  7.2 2.2 %collective-permute-start.1 = (f32[2,4]{1,0:T(2,128)S(1)}, f32[2,4]{1,0:T(2,128)S(1)}, u32[]{:S(2)}, u32[]{:S(2)}) collective-permute-start(f32[2,4]{1,0:T(2,128)S(1)} %pad_maximum_fusion.2), channel_id=1, source_target_pairs={{0,2},{1,3},{2,0},{3,1},{4,6},{5,7},{6,4},{7,5},{8,10},{9,11},{10,... | collective-permute-start | bytes 104 | tf_op jit(solution)/shard_map/ppermute | solution.py:9
  9.4 1.6 %collective-permute-done.1 = f32[2,4]{1,0:T(2,128)S(1)} collective-permute-done((f32[2,4]{1,0:T(2,128)S(1)}, f32[2,4]{1,0:T(2,128)S(1)}, u32[]{:S(2)}, u32[]{:S(2)}) %collective-permute-start.1) | collective-permute-done | bytes 64 | tf_op jit(solution)/shard_map/ppermute | solution.py:9
  10.9 3.1 %collective-permute-start.2 = (f32[2,4]{1,0:T(2,128)S(1)}, f32[2,4]{1,0:T(2,128)S(1)}, u32[]{:S(2)}, u32[]{:S(2)}) collective-permute-start(f32[2,4]{1,0:T(2,128)S(1)} %pad_maximum_fusion.3), channel_id=1, source_target_pairs={{0,4},{1,5},{2,6},{3,7},{4,0},{5,1},{6,2},{7,3},{8,12},{9,13},{10,... | collective-permute-start | bytes 104 | tf_op jit(solution)/shard_map/ppermute | solution.py:9
  14.0 1.6 %collective-permute-done.2 = f32[2,4]{1,0:T(2,128)S(1)} collective-permute-done((f32[2,4]{1,0:T(2,128)S(1)}, f32[2,4]{1,0:T(2,128)S(1)}, u32[]{:S(2)}, u32[]{:S(2)}) %collective-permute-start.2) | collective-permute-done | bytes 64 | tf_op jit(solution)/shard_map/ppermute | solution.py:9
  15.6 4.2 %multiply_reduce_fusion = (f32[64,4096]{1,0:T(8,128)S(1)}, f32[64,4096]{1,0:T(8,128)S(1)}) fusion(bf16[4,64,4096]{2,1,0:T(8,128)(2,1)} %param.2, f32[4]{0:T(128)S(1)} %get-tuple-element.9, f32[4,64,4096]{2,1,0:T(8,128)} %param.3, f32[4]{0:T(128)S(1)} %get-tuple-element.10), kind=kLoop, calls=%fused_computation | loop fusion | flops 6815744 | bytes 8388640 | tf_op jit(solution)/shard_map/reduce_sum | solution.py:40
  19.9 1.1 %broadcast_select_fusion = f32[2,32,4096]{2,1,0:T(8,128)} fusion(pred[]{:T(512)S(6)} %ne.8, f32[1,64,4096]{2,1,0:T(8,128)S(1)} %bitcast.35, f32[1,64,4096]{2,1,0:T(8,128)S(1)} %bitcast.33), kind=kLoop, calls=%fused_computation.9 | loop fusion | flops 786432 | bytes 3145729 | tf_op jit(solution)/shard_map/jit(_where)/select_n | solution.py:32
  21.0 0.0 collective-permute-start.3
  21.0 2.9 %collective-permute-done.3 = f32[2,32,4096]{2,1,0:T(8,128)S(1)} collective-permute-done((f32[2,32,4096]{2,1,0:T(8,128)}, f32[2,32,4096]{2,1,0:T(8,128)S(1)}, u32[]{:S(2)}, u32[]{:S(2)}) %collective-permute-start.3) | collective-permute-done | bytes 1048608 | tf_op jit(solution)/shard_map/ppermute | solution.py:9
  23.8 0.1 select_add_fusion
  24.0 0.1 slice_select_fusion
  24.0 1.9 %collective-permute-start.4 = (f32[2,16,4096]{2,1,0:T(8,128)S(1)}, f32[2,16,4096]{2,1,0:T(8,128)S(1)}, u32[]{:S(2)}, u32[]{:S(2)}) collective-permute-start(f32[2,16,4096]{2,1,0:T(8,128)S(1)} %slice_select_fusion), channel_id=1, source_target_pairs={{0,16},{8,24},{16,0},{24,8},{1,17},{9,25},{17,1},{25,9},{2,18},{10... | collective-permute-start | bytes 1572872 | tf_op jit(solution)/shard_map/ppermute | solution.py:9
  26.0 12.2 %collective-permute-done.4 = f32[2,16,4096]{2,1,0:T(8,128)S(1)} collective-permute-done((f32[2,16,4096]{2,1,0:T(8,128)S(1)}, f32[2,16,4096]{2,1,0:T(8,128)S(1)}, u32[]{:S(2)}, u32[]{:S(2)}) %collective-permute-start.4) | collective-permute-done | bytes 524320 | tf_op jit(solution)/shard_map/ppermute | solution.py:9
  38.2 0.1 select_add_fusion.1
  38.4 1.8 %collective-permute-start.5 = (bf16[16,4096]{1,0:T(8,128)(2,1)S(1)}, bf16[16,4096]{1,0:T(8,128)(2,1)S(1)}, u32[]{:S(2)}, u32[]{:S(2)}) collective-permute-start(bf16[16,4096]{1,0:T(8,128)(2,1)S(1)} %fusion.2), channel_id=1, source_target_pairs={{0,16},{8,24},{16,0},{24,8},{1,17},{9,25},{17,1},{25,9},{2,18},{10... | collective-permute-start | bytes 393224 | tf_op jit(solution)/shard_map/ppermute | solution.py:9
  40.2 3.2 %collective-permute-done.5 = bf16[16,4096]{1,0:T(8,128)(2,1)S(1)} collective-permute-done((bf16[16,4096]{1,0:T(8,128)(2,1)S(1)}, bf16[16,4096]{1,0:T(8,128)(2,1)S(1)}, u32[]{:S(2)}, u32[]{:S(2)}) %collective-permute-start.5) | collective-permute-done | bytes 131104 | tf_op jit(solution)/shard_map/ppermute | solution.py:9
  43.4 0.1 collective-permute-start.6
  43.5 1.5 %collective-permute-done.6 = bf16[32,4096]{1,0:T(8,128)(2,1)S(1)} collective-permute-done((bf16[32,4096]{1,0:T(8,128)(2,1)S(1)}, bf16[32,4096]{1,0:T(8,128)(2,1)S(1)}, u32[]{:S(2)}, u32[]{:S(2)}) %collective-permute-start.6) | collective-permute-done | bytes 262176 | tf_op jit(solution)/shard_map/ppermute | solution.py:9
  45.0 0.9 %maximum_select_fusion = bf16[64,4096]{1,0:T(8,128)(2,1)} fusion(bf16[32,4096]{1,0:T(8,128)(2,1)S(1)} %maximum_select_fusion.1, bf16[32,4096]{1,0:T(8,128)(2,1)S(1)} %collective-permute-done.6, pred[]{:T(512)S(6)} %ne.8), kind=kLoop, calls=%fused_computation.7 | loop fusion | flops 2359296 | bytes 1048577 | tf_op jit(solution)/shard_map/jit(_where)/select_n | solution.py:51
  (8 shorter events, 0.1 us)
Async XLA Ops:
  2.6 4.6 %collective-permute-start = (f32[2,4]{1,0:T(2,128)S(1)}, f32[2,4]{1,0:T(2,128)S(1)}, u32[]{:S(2)}, u32[]{:S(2)}) collective-permute-start(f32[2,4]{1,0:T(2,128)S(1)} %pad_maximum_fusion.1), channel_id=1, source_target_pairs={{0,1},{1,0},{2,3},{3,2},{4,5},{5,4},{6,7},{7,6},{8,9},{9,8},{10,11... | collective-permute-start | bytes 104 | tf_op jit(solution)/shard_map/ppermute | solution.py:9
  7.2 3.7 %collective-permute-start.1 = (f32[2,4]{1,0:T(2,128)S(1)}, f32[2,4]{1,0:T(2,128)S(1)}, u32[]{:S(2)}, u32[]{:S(2)}) collective-permute-start(f32[2,4]{1,0:T(2,128)S(1)} %pad_maximum_fusion.2), channel_id=1, source_target_pairs={{0,2},{1,3},{2,0},{3,1},{4,6},{5,7},{6,4},{7,5},{8,10},{9,11},{10,... | collective-permute-start | bytes 104 | tf_op jit(solution)/shard_map/ppermute | solution.py:9
  10.9 4.7 %collective-permute-start.2 = (f32[2,4]{1,0:T(2,128)S(1)}, f32[2,4]{1,0:T(2,128)S(1)}, u32[]{:S(2)}, u32[]{:S(2)}) collective-permute-start(f32[2,4]{1,0:T(2,128)S(1)} %pad_maximum_fusion.3), channel_id=1, source_target_pairs={{0,4},{1,5},{2,6},{3,7},{4,0},{5,1},{6,2},{7,3},{8,12},{9,13},{10,... | collective-permute-start | bytes 104 | tf_op jit(solution)/shard_map/ppermute | solution.py:9
  21.0 2.9 %collective-permute-start.3 = (f32[2,32,4096]{2,1,0:T(8,128)}, f32[2,32,4096]{2,1,0:T(8,128)S(1)}, u32[]{:S(2)}, u32[]{:S(2)}) collective-permute-start(f32[2,32,4096]{2,1,0:T(8,128)} %broadcast_select_fusion), channel_id=1, source_target_pairs={{0,8},{8,0},{16,24},{24,16},{1,9},{9,1},{17,25},{25,17},{2,10},{10... | collective-permute-start | bytes 3145736 | tf_op jit(solution)/shard_map/ppermute | solution.py:9
  24.0 14.1 %collective-permute-start.4 = (f32[2,16,4096]{2,1,0:T(8,128)S(1)}, f32[2,16,4096]{2,1,0:T(8,128)S(1)}, u32[]{:S(2)}, u32[]{:S(2)}) collective-permute-start(f32[2,16,4096]{2,1,0:T(8,128)S(1)} %slice_select_fusion), channel_id=1, source_target_pairs={{0,16},{8,24},{16,0},{24,8},{1,17},{9,25},{17,1},{25,9},{2,18},{10... | collective-permute-start | bytes 1572872 | tf_op jit(solution)/shard_map/ppermute | solution.py:9
  38.4 5.0 %collective-permute-start.5 = (bf16[16,4096]{1,0:T(8,128)(2,1)S(1)}, bf16[16,4096]{1,0:T(8,128)(2,1)S(1)}, u32[]{:S(2)}, u32[]{:S(2)}) collective-permute-start(bf16[16,4096]{1,0:T(8,128)(2,1)S(1)} %fusion.2), channel_id=1, source_target_pairs={{0,16},{8,24},{16,0},{24,8},{1,17},{9,25},{17,1},{25,9},{2,18},{10... | collective-permute-start | bytes 393224 | tf_op jit(solution)/shard_map/ppermute | solution.py:9
  43.4 1.6 %collective-permute-start.6 = (bf16[32,4096]{1,0:T(8,128)(2,1)S(1)}, bf16[32,4096]{1,0:T(8,128)(2,1)S(1)}, u32[]{:S(2)}, u32[]{:S(2)}) collective-permute-start(bf16[32,4096]{1,0:T(8,128)(2,1)S(1)} %maximum_select_fusion.1), channel_id=1, source_target_pairs={{0,8},{8,0},{16,24},{24,16},{1,9},{9,1},{17,25},{25,17},{2,10},{10... | collective-permute-start | bytes 786440 | tf_op jit(solution)/shard_map/ppermute | solution.py:9

commit v2 on v0

v2 whole, which is shorter than its diff:
```python
import functools

import jax
import jax.numpy as jnp
from jax import lax
from jax.experimental import pallas as pl
from jax.experimental.pallas import tpu as pltpu
from jax.sharding import PartitionSpec as P

CHUNKS = 2
STEP = 512
PIECES = 2
COST = 100
PARAMS = pltpu.CompilerParams(vmem_limit_bytes=16 * 1024 * 1024)
VMEM = pl.BlockSpec(memory_space=pltpu.VMEM)
SMEM = pl.BlockSpec(memory_space=pltpu.SMEM)
HBM = pl.BlockSpec(memory_space=pltpu.HBM)


def swap(value, axis, bit):
    size = lax.axis_size(axis)
    return lax.ppermute(value, axis, [(i, i ^ bit) for i in range(size)])


def bits_of(axis):
    size = lax.axis_size(axis)
    return [1 << k for k in range(size.bit_length() - 1)]


def side(axis, bit):
    return ((lax.axis_index(axis) & bit) != 0).astype(jnp.int32).reshape(1)


def stats_kernel(fisher_ref, stats_ref, fisher_out, sems):
    tasks, rows, width = fisher_out.shape
    step = rows // PIECES
    loads = []
    for task in range(tasks):
        for piece in range(PIECES):
            at = (task, pl.ds(piece * step, step))
            loads.append(pltpu.make_async_copy(fisher_ref.at[at], fisher_out.at[at], sems.at[len(loads)]))
    for load in loads:
        load.start()
    for task in range(tasks):
        top = added = None
        for piece in range(PIECES):
            loads[task * PIECES + piece].wait()
            for row in range(piece * step, piece * step + step, 8):
                for col in range(0, width, 1024):
                    block = fisher_out[task, row : row + 8, col : col + 1024]
                    top = block if top is None else jnp.maximum(top, block)
                    added = block if added is None else added + block
        stats_ref[task : task + 1] = jnp.full((1, 128), jnp.max(top), jnp.float32)
        stats_ref[tasks + task : tasks + task + 1] = jnp.full((1, 128), jnp.sum(added), jnp.float32)


def local_stats(fisher):
    tasks = fisher.shape[0]
    return pl.pallas_call(
        stats_kernel,
        in_specs=[HBM],
        out_specs=VMEM,
        out_shape=pltpu.VMEM((2 * tasks, 128), jnp.float32),
        scratch_shapes=[pltpu.VMEM(fisher.shape, jnp.float32), pltpu.SemaphoreType.DMA((tasks * PIECES,))],
        name="local_stats",
    )(fisher)


def joined(one_ref, two_ref):
    tasks = one_ref.shape[0] // 2
    one, two = one_ref[...], two_ref[...]
    return jnp.maximum(one[:tasks], two[:tasks]), one[tasks:] + two[tasks:]


def join_kernel(one_ref, two_ref, out_ref):
    tasks = one_ref.shape[0] // 2
    out_ref[:tasks], out_ref[tasks:] = joined(one_ref, two_ref)


def join(one, two):
    return pl.pallas_call(
        join_kernel, in_specs=[VMEM] * 2, out_specs=VMEM, out_shape=pltpu.VMEM(one.shape, one.dtype), compiler_params=PARAMS, name="join"
    )(one, two)


def coef_kernel(one_ref, two_ref, out_ref, *, count):
    peak, total = joined(one_ref, two_ref)
    scale = count / total
    factor = scale * peak
    for k, value in enumerate([scale, 0.002 * factor, 0.25 * factor]):
        for task in range(value.shape[0]):
            out_ref[k * value.shape[0] + task, 0] = value[task, 0]


def coefs(one, two, count):
    kind = pltpu.SMEM((3 * one.shape[0] // 2, 1), jnp.float32)
    return pl.pallas_call(
        functools.partial(coef_kernel, count=count),
        in_specs=[VMEM] * 2,
        out_specs=SMEM,
        out_shape=kind,
        compiler_params=PARAMS,
        name="coefs",
    )(one, two)


def weigh_kernel(half_ref, stats_ref, fisher_hbm, params_hbm, after_ref, out_ref, fisher_ref, params_ref, sems, *, col):
    tasks, rows, cols = fisher_ref.shape
    step = min(cols, STEP)
    start = pl.ds(pl.multiple_of(half_ref[0] * rows, rows), rows)
    loads = []
    for piece in range(cols // step):
        source, target = pl.ds(col + piece * step, step), pl.ds(piece * step, step)
        pair = [
            pltpu.make_async_copy(hbm.at[:, start, source], ref.at[:, :, target], sems.at[k, piece])
            for k, (hbm, ref) in enumerate([(fisher_hbm, fisher_ref), (params_hbm, params_ref)])
        ]
        for copy in pair:
            copy.start()
        loads.append(pair)
    coef = [tuple(stats_ref[k * tasks + task, 0] for k in range(3)) for task in range(tasks)]
    for piece in range(cols // step):
        for copy in loads[piece]:
            copy.wait()
        for row in range(0, rows, 8):
            place = (slice(row, row + 8), slice(piece * step, piece * step + step))
            numer = denom = None
            for task in range(tasks):
                by, least, most = coef[task]
                weight = jnp.minimum(jnp.maximum(fisher_ref[(task,) + place] * by, least), most)
                term = weight * params_ref[(task,) + place].astype(jnp.float32)
                numer = term if task == 0 else numer + term
                denom = weight if task == 0 else denom + weight
            out_ref[(0,) + place] = numer
            out_ref[(1,) + place] = denom


def weighted(params, fisher, one, block, rows, col, cols, after, name):
    tasks = fisher.shape[0]
    return pl.pallas_call(
        functools.partial(weigh_kernel, col=col),
        in_specs=[SMEM, SMEM, HBM, HBM, SMEM],
        out_specs=VMEM,
        out_shape=pltpu.VMEM((2, rows, cols), jnp.float32),
        scratch_shapes=[
            pltpu.VMEM((tasks, rows, cols), jnp.float32),
            pltpu.VMEM((tasks, rows, cols), jnp.bfloat16),
            pltpu.SemaphoreType.DMA((2, cols // min(cols, STEP))),
        ],
        cost_estimate=pl.CostEstimate(flops=8 * tasks * rows * cols * COST, transcendentals=0, bytes_accessed=6 * tasks * rows * cols),
        name=name,
    )(block, one, fisher, params, after)


def split_kernel(upper_ref, one_ref, two_ref, send_ref, keep_ref, token_ref):
    token_ref[0] = upper_ref[0]
    size = send_ref.shape[1]
    mine = pl.multiple_of(upper_ref[0] * size, size)
    theirs = pl.multiple_of((1 - upper_ref[0]) * size, size)
    for k in range(2):
        send_ref[k] = one_ref[k, pl.ds(theirs, size)] + two_ref[k, pl.ds(theirs, size)]
        keep_ref[k] = one_ref[k, pl.ds(mine, size)] + two_ref[k, pl.ds(mine, size)]


def split(upper, one, two):
    kind = pltpu.VMEM((2, one.shape[1] // 2, one.shape[2]), one.dtype)
    return pl.pallas_call(
        split_kernel, in_specs=[SMEM, VMEM, VMEM], out_specs=[VMEM, VMEM, SMEM], out_shape=[kind, kind, pltpu.SMEM((1,), jnp.int32)], compiler_params=PARAMS, name="split"
    )(upper, one, two)


def merge_kernel(one_ref, two_ref, out_ref):
    out_ref[...] = ((one_ref[0] + two_ref[0]) / (one_ref[1] + two_ref[1])).astype(out_ref.dtype)


def merge(one, two):
    kind = pltpu.VMEM(one.shape[1:], jnp.bfloat16)
    return pl.pallas_call(
        merge_kernel, in_specs=[VMEM] * 2, out_specs=VMEM, out_shape=kind, compiler_params=PARAMS, name="merge"
    )(one, two)


def stacked(upper, mine, other):
    return jnp.where(upper[0] != 0, jnp.concatenate([other, mine]), jnp.concatenate([mine, other]))


def local(params, fisher):
    tasks, rows, width = fisher.shape
    count = float(rows * lax.axis_size("param") * width)
    one = local_stats(fisher)
    *early, final = bits_of("param")
    for bit in early:
        one = join(one, swap(one, "param", bit))
    two = swap(one, "param", final)
    first, *rest = bits_of("task")
    half, cols = rows // 2, width // CHUNKS
    core = side("task", first)
    uppers = {bit: side("task", bit) for bit in rest}
    after, merged = core, []
    coef = coefs(one, two, count)
    for chunk in range(CHUNKS):
        send = weighted(params, fisher, coef, 1 - core, half, chunk * cols, cols, after, "weigh_send")
        keep = weighted(params, fisher, coef, core, half, chunk * cols, cols, after, "weigh_keep")
        other = swap(send, "task", first)
        for bit in rest:
            send, keep, after = split(uppers[bit], keep, other)
            other = swap(send, "task", bit)
        out = merge(keep, other)
        for bit in reversed(rest):
            out = stacked(uppers[bit], out, swap(out, "task", bit))
        merged.append(out)
    out = jnp.concatenate(merged, axis=1)
    return stacked(core, out, swap(out, "task", first))


def solution(mesh):
    in_specs = (P("task", "param", None), P("task", "param", None))
    out_specs = P("param", None)
    return jax.shard_map(local, mesh=mesh, in_specs=in_specs, out_specs=out_specs, check_vma=False)
```

time: 98 us -> 42.6 us (0.43)
  waiting for transfers between devices: 48.8 us -> 18.1 us
  blocking collectives: 23.1 us -> 0 us
  starting transfers between devices: 0.01 us -> 14.5 us
  between operations: 14.1 us -> 0.13 us
  other arithmetic: 10.2 us -> 0.95 us
  Pallas kernels: 0 us -> 8.64 us
  local copies, waits for them, and re-layouts: 1.43 us -> 0 us
    psum x1 -> x0, waiting for transfers between devices: 48.8 us -> none  [local(): numer, denom = lax.psum((numer, denom), 'task')]
    unnamed x1 -> x0, blocking collectives: 23.1 us -> none
    ppermute x0 -> x10, waiting for transfers between devices: none -> 18.1 us  [swap(): return lax.ppermute(value, axis, [(i, i ^ bit) for i in range(size)])]
    ppermute x0 -> x10, starting transfers between devices: none -> 14.5 us  [swap(): return lax.ppermute(value, axis, [(i, i ^ bit) for i in range(size)])]
    pallas_call x0 -> x12, Pallas kernels: none -> 8.64 us  [the longest x4 6.03 us: weighted(): pl.pallas_call(functools.partial(weigh_kernel, col=col), in_specs=[SMEM,...]
    reduce_sum x2 -> x0, other arithmetic: 7.65 us -> none  [the longest x1 4.9 us: local(): denom = jnp.sum(weight, axis=0)]
    convert_element_type x1 -> x0, other arithmetic: 2.48 us -> none  [local(): return (numer / denom).astype(jnp.bfloat16)]
    unnamed x9 -> x0, local copies, waits for them, and re-layouts: 1.12 us -> none
  transfers between devices with their start and end apart: 1 -> 10, of which waited for: 1 -> 8; matrix products, arithmetic and copies ran while one was open for 0% -> 0% of each run, Pallas kernels for 0% -> 7%
where the time goes in v2:
time: 42.6 us; the launch traced here: 42.4 us
  waiting for transfers between devices  18.1 us (42%)
  starting transfers between devices  14.5 us (34%)
  Pallas kernels  8.64 us (20%)
  other arithmetic  0.95 us (2%)
    ppermute x10, waiting for transfers between devices, swap(): return lax.ppermute(value, axis, [(i, i ^ bit) for i in range(size)])  18.1 us
    ppermute x10, starting transfers between devices, swap(): return lax.ppermute(value, axis, [(i, i ^ bit) for i in range(size)])  14.5 us
    pallas_call x4, Pallas kernels, weighted(): pl.pallas_call(functools.partial(weigh_kernel, col=col), in_specs=[SMEM,...  6.03 us
    pallas_call x1, Pallas kernels, local_stats(): pl.pallas_call(stats_kernel, in_specs=[HBM], out_specs=VMEM, out_shape=pl...  2.37 us
    select_n x3, other arithmetic, stacked(): jnp.where(upper[0] != 0, jnp.concatenate([other, mine]), jnp.concatenate(...  0.93 us
  transfers between devices with their start and end apart: 10, of which 8 were waited for; matrix products, arithmetic and copies ran while one was open for 0% of the time, Pallas kernels for 7%

profile of v2, /device:TPU:0, one launch (start us, length us, event | category | flops | bytes accessed | tf_op | source)
XLA Modules:
  0.0 42.4 jit_solution(15915264451904955895)
XLA Ops:
  0.0 2.4 %local_stats.1.one_ref = f32[8,128]{1,0:T(8,128)S(1)} custom-call(f32[4,64,4096]{2,1,0:T(8,128)} %fisher_hbm.7), custom_call_target="tpu_custom_call" | custom-call | tf_op jit(solution)/shard_map/local_stats/pallas_call | solution.py:59
  2.4 3.0 %collective-permute-start = (f32[8,128]{1,0:T(8,128)S(1)}, f32[8,128]{1,0:T(8,128)S(1)}, u32[]{:S(2)}, u32[]{:S(2)}) collective-permute-start(f32[8,128]{1,0:T(8,128)S(1)} %local_stats.1.one_ref), channel_id=1, source_target_pairs={{0,1},{1,0},{2,3},{3,2},{4,5},{5,4},{6,7},{7,6},{8,9},{9,8},{10,11... | collective-permute-start | bytes 12296 | tf_op jit(solution)/shard_map/ppermute | solution.py:22
  5.4 1.6 %collective-permute-done.two_ref = f32[8,128]{1,0:T(8,128)S(1)} collective-permute-done((f32[8,128]{1,0:T(8,128)S(1)}, f32[8,128]{1,0:T(8,128)S(1)}, u32[]{:S(2)}, u32[]{:S(2)}) %collective-permute-start) | collective-permute-done | bytes 4128 | tf_op jit(solution)/shard_map/ppermute | solution.py:22
  7.0 2.1 %collective-permute-start.1 = (f32[8,128]{1,0:T(8,128)S(1)}, f32[8,128]{1,0:T(8,128)S(1)}, u32[]{:S(2)}, u32[]{:S(2)}) collective-permute-start(f32[8,128]{1,0:T(8,128)S(1)} %join.2.one_ref), channel_id=1, source_target_pairs={{0,2},{1,3},{2,0},{3,1},{4,6},{5,7},{6,4},{7,5},{8,10},{9,11},{10,... | collective-permute-start | bytes 12296 | tf_op jit(solution)/shard_map/ppermute | solution.py:22
  9.1 1.6 %collective-permute-done.1.two_ref = f32[8,128]{1,0:T(8,128)S(1)} collective-permute-done((f32[8,128]{1,0:T(8,128)S(1)}, f32[8,128]{1,0:T(8,128)S(1)}, u32[]{:S(2)}, u32[]{:S(2)}) %collective-permute-start.1) | collective-permute-done | bytes 4128 | tf_op jit(solution)/shard_map/ppermute | solution.py:22
  10.7 3.0 %collective-permute-start.2 = (f32[8,128]{1,0:T(8,128)S(1)}, f32[8,128]{1,0:T(8,128)S(1)}, u32[]{:S(2)}, u32[]{:S(2)}) collective-permute-start(f32[8,128]{1,0:T(8,128)S(1)} %join.3.one_ref), channel_id=1, source_target_pairs={{0,4},{1,5},{2,6},{3,7},{4,0},{5,1},{6,2},{7,3},{8,12},{9,13},{10,... | collective-permute-start | bytes 12296 | tf_op jit(solution)/shard_map/ppermute | solution.py:22
  13.7 1.6 %collective-permute-done.2.two_ref = f32[8,128]{1,0:T(8,128)S(1)} collective-permute-done((f32[8,128]{1,0:T(8,128)S(1)}, f32[8,128]{1,0:T(8,128)S(1)}, u32[]{:S(2)}, u32[]{:S(2)}) %collective-permute-start.2) | collective-permute-done | bytes 4128 | tf_op jit(solution)/shard_map/ppermute | solution.py:22
  15.4 1.5 %weigh_send.2 = f32[2,32,2048]{2,1,0:T(8,128)S(1)} custom-call(s32[1]{0:T(128)S(6)} %sub.4.half_ref, f32[12,1]{1,0:T(8,128)S(4)} %coefs.1.stats_ref, f32[4,64,4096]{2,1,0:T(8,128)} %fisher_hbm.7, bf16[4,64,4096]{2,1,0:T(8,128)(2,1)} %params_hbm.7, s32[1]{0:T(128)} %bitcast.1.half_ref.after_ref), custom_call_target="tpu_custom_call" | custom-call | flops 209715200 | bytes 1572864 | tf_op jit(solution)/shard_map/weigh_send/pallas_call | solution.py:140
  16.9 0.1 collective-permute-start.3
  17.0 1.5 %weigh_keep.2.one_ref = f32[2,32,2048]{2,1,0:T(8,128)S(1)} custom-call(s32[1]{0:T(128)} %bitcast.1.half_ref.after_ref, f32[12,1]{1,0:T(8,128)S(4)} %coefs.1.stats_ref, f32[4,64,4096]{2,1,0:T(8,128)} %fisher_hbm.7, bf16[4,64,4096]{2,1,0:T(8,128)(2,1)} %params_hbm.7, s32[1]{0:T(128)} %bitcast.1.half_ref.after_ref), custom_call_target="tpu_custom_call" | custom-call | flops 209715200 | bytes 1572864 | tf_op jit(solution)/shard_map/weigh_keep/pallas_call | solution.py:140
  18.5 0.4 collective-permute-done.3.two_ref
  18.9 1.5 %weigh_send.3 = f32[2,32,2048]{2,1,0:T(8,128)S(1)} custom-call(s32[1]{0:T(128)S(6)} %sub.4.half_ref, f32[12,1]{1,0:T(8,128)S(4)} %coefs.1.stats_ref, f32[4,64,4096]{2,1,0:T(8,128)} %fisher_hbm.7, bf16[4,64,4096]{2,1,0:T(8,128)(2,1)} %params_hbm.7, s32[1]{0:T(128)S(4)} %get-tuple-element.12.after_ref), custom_call_target="tpu_custom_call" | custom-call | flops 209715200 | bytes 1572864 | tf_op jit(solution)/shard_map/weigh_send/pallas_call | solution.py:140
  20.5 0.2 collective-permute-start.6
  20.7 1.9 %collective-permute-start.4 = (f32[2,16,2048]{2,1,0:T(8,128)S(1)}, f32[2,16,2048]{2,1,0:T(8,128)S(1)}, u32[]{:S(2)}, u32[]{:S(2)}) collective-permute-start(f32[2,16,2048]{2,1,0:T(8,128)S(1)} %get-tuple-element.11), channel_id=1, source_target_pairs={{0,16},{8,24},{16,0},{24,8},{1,17},{9,25},{17,1},{25,9},{2,18},{10... | collective-permute-start | bytes 786440 | tf_op jit(solution)/shard_map/ppermute | solution.py:22
  22.5 1.5 %weigh_keep.3.one_ref = f32[2,32,2048]{2,1,0:T(8,128)S(1)} custom-call(s32[1]{0:T(128)} %bitcast.1.half_ref.after_ref, f32[12,1]{1,0:T(8,128)S(4)} %coefs.1.stats_ref, f32[4,64,4096]{2,1,0:T(8,128)} %fisher_hbm.7, bf16[4,64,4096]{2,1,0:T(8,128)(2,1)} %params_hbm.7, s32[1]{0:T(128)S(4)} %get-tuple-element.12.after_ref), custom_call_target="tpu_custom_call" | custom-call | flops 209715200 | bytes 1572864 | tf_op jit(solution)/shard_map/weigh_keep/pallas_call | solution.py:140
  24.1 0.3 collective-permute-start.7
  24.4 5.4 %collective-permute-done.4.two_ref = f32[2,16,2048]{2,1,0:T(8,128)S(1)} collective-permute-done((f32[2,16,2048]{2,1,0:T(8,128)S(1)}, f32[2,16,2048]{2,1,0:T(8,128)S(1)}, u32[]{:S(2)}, u32[]{:S(2)}) %collective-permute-start.4) | collective-permute-done | bytes 262176 | tf_op jit(solution)/shard_map/ppermute | solution.py:22
  29.9 1.9 %collective-permute-start.5 = (bf16[16,2048]{1,0:T(8,128)(2,1)S(1)}, bf16[16,2048]{1,0:T(8,128)(2,1)S(1)}, u32[]{:S(2)}, u32[]{:S(2)}) collective-permute-start(bf16[16,2048]{1,0:T(8,128)(2,1)S(1)} %merge.2), channel_id=1, source_target_pairs={{0,16},{8,24},{16,0},{24,8},{1,17},{9,25},{17,1},{25,9},{2,18},{10... | collective-permute-start | bytes 196616 | tf_op jit(solution)/shard_map/ppermute | solution.py:22
  31.8 3.7 %collective-permute-done.7.two_ref = f32[2,16,2048]{2,1,0:T(8,128)S(1)} collective-permute-done((f32[2,16,2048]{2,1,0:T(8,128)S(1)}, f32[2,16,2048]{2,1,0:T(8,128)S(1)}, u32[]{:S(2)}, u32[]{:S(2)}) %collective-permute-start.7) | collective-permute-done | bytes 262176 | tf_op jit(solution)/shard_map/ppermute | solution.py:22
  35.5 1.9 %collective-permute-start.8 = (bf16[16,2048]{1,0:T(8,128)(2,1)S(1)}, bf16[16,2048]{1,0:T(8,128)(2,1)S(1)}, u32[]{:S(2)}, u32[]{:S(2)}) collective-permute-start(bf16[16,2048]{1,0:T(8,128)(2,1)S(1)} %merge.3), channel_id=1, source_target_pairs={{0,16},{8,24},{16,0},{24,8},{1,17},{9,25},{17,1},{25,9},{2,18},{10... | collective-permute-start | bytes 196616 | tf_op jit(solution)/shard_map/ppermute | solution.py:22
  37.4 2.4 %collective-permute-done.8 = bf16[16,2048]{1,0:T(8,128)(2,1)S(1)} collective-permute-done((bf16[16,2048]{1,0:T(8,128)(2,1)S(1)}, bf16[16,2048]{1,0:T(8,128)(2,1)S(1)}, u32[]{:S(2)}, u32[]{:S(2)}) %collective-permute-start.8) | collective-permute-done | bytes 65568 | tf_op jit(solution)/shard_map/ppermute | solution.py:22
  39.9 0.1 collective-permute-start.9
  40.0 1.5 %collective-permute-done.9 = bf16[32,4096]{1,0:T(8,128)(2,1)S(1)} collective-permute-done((bf16[32,4096]{1,0:T(8,128)(2,1)S(1)}, bf16[32,4096]{1,0:T(8,128)(2,1)S(1)}, u32[]{:S(2)}, u32[]{:S(2)}) %collective-permute-start.9) | collective-permute-done | bytes 262176 | tf_op jit(solution)/shard_map/ppermute | solution.py:22
  41.5 0.9 %maximum_select_fusion = bf16[64,4096]{1,0:T(8,128)(2,1)} fusion(bf16[32,2048]{1,0:T(8,128)(2,1)S(1)} %maximum_select_fusion.2, bf16[32,2048]{1,0:T(8,128)(2,1)S(1)} %maximum_select_fusion.1, bf16[32,4096]{1,0:T(8,128)(2,1)S(1)} %collective-permute-done.9, pred[]{:T(512)S(6)} %ne.14), kind=kLoop, calls=%fused_computation | loop fusion | flops 3407872 | bytes 1048577 | tf_op jit(solution)/shard_map/jit(_where)/select_n | solution.py:184
  (12 shorter events, 0.3 us)
Async XLA Ops:
  2.4 4.6 %collective-permute-start = (f32[8,128]{1,0:T(8,128)S(1)}, f32[8,128]{1,0:T(8,128)S(1)}, u32[]{:S(2)}, u32[]{:S(2)}) collective-permute-start(f32[8,128]{1,0:T(8,128)S(1)} %local_stats.1.one_ref), channel_id=1, source_target_pairs={{0,1},{1,0},{2,3},{3,2},{4,5},{5,4},{6,7},{7,6},{8,9},{9,8},{10,11... | collective-permute-start | bytes 12296 | tf_op jit(solution)/shard_map/ppermute | solution.py:22
  7.0 3.7 %collective-permute-start.1 = (f32[8,128]{1,0:T(8,128)S(1)}, f32[8,128]{1,0:T(8,128)S(1)}, u32[]{:S(2)}, u32[]{:S(2)}) collective-permute-start(f32[8,128]{1,0:T(8,128)S(1)} %join.2.one_ref), channel_id=1, source_target_pairs={{0,2},{1,3},{2,0},{3,1},{4,6},{5,7},{6,4},{7,5},{8,10},{9,11},{10,... | collective-permute-start | bytes 12296 | tf_op jit(solution)/shard_map/ppermute | solution.py:22
  10.7 4.6 %collective-permute-start.2 = (f32[8,128]{1,0:T(8,128)S(1)}, f32[8,128]{1,0:T(8,128)S(1)}, u32[]{:S(2)}, u32[]{:S(2)}) collective-permute-start(f32[8,128]{1,0:T(8,128)S(1)} %join.3.one_ref), channel_id=1, source_target_pairs={{0,4},{1,5},{2,6},{3,7},{4,0},{5,1},{6,2},{7,3},{8,12},{9,13},{10,... | collective-permute-start | bytes 12296 | tf_op jit(solution)/shard_map/ppermute | solution.py:22
  16.9 2.0 %collective-permute-start.3 = (f32[2,32,2048]{2,1,0:T(8,128)S(1)}, f32[2,32,2048]{2,1,0:T(8,128)S(1)}, u32[]{:S(2)}, u32[]{:S(2)}) collective-permute-start(f32[2,32,2048]{2,1,0:T(8,128)S(1)} %weigh_send.2), channel_id=1, source_target_pairs={{0,8},{8,0},{16,24},{24,16},{1,9},{9,1},{17,25},{25,17},{2,10},{10... | collective-permute-start | bytes 1572872 | tf_op jit(solution)/shard_map/ppermute | solution.py:22
  20.5 3.6 %collective-permute-start.6 = (f32[2,32,2048]{2,1,0:T(8,128)S(1)}, f32[2,32,2048]{2,1,0:T(8,128)S(1)}, u32[]{:S(2)}, u32[]{:S(2)}) collective-permute-start(f32[2,32,2048]{2,1,0:T(8,128)S(1)} %weigh_send.3), channel_id=1, source_target_pairs={{0,8},{8,0},{16,24},{24,16},{1,9},{9,1},{17,25},{25,17},{2,10},{10... | collective-permute-start | bytes 1572872 | tf_op jit(solution)/shard_map/ppermute | solution.py:22
  20.7 9.2 %collective-permute-start.4 = (f32[2,16,2048]{2,1,0:T(8,128)S(1)}, f32[2,16,2048]{2,1,0:T(8,128)S(1)}, u32[]{:S(2)}, u32[]{:S(2)}) collective-permute-start(f32[2,16,2048]{2,1,0:T(8,128)S(1)} %get-tuple-element.11), channel_id=1, source_target_pairs={{0,16},{8,24},{16,0},{24,8},{1,17},{9,25},{17,1},{25,9},{2,18},{10... | collective-permute-start | bytes 786440 | tf_op jit(solution)/shard_map/ppermute | solution.py:22
  24.1 11.4 %collective-permute-start.7 = (f32[2,16,2048]{2,1,0:T(8,128)S(1)}, f32[2,16,2048]{2,1,0:T(8,128)S(1)}, u32[]{:S(2)}, u32[]{:S(2)}) collective-permute-start(f32[2,16,2048]{2,1,0:T(8,128)S(1)} %get-tuple-element.14), channel_id=1, source_target_pairs={{0,16},{8,24},{16,0},{24,8},{1,17},{9,25},{17,1},{25,9},{2,18},{10... | collective-permute-start | bytes 786440 | tf_op jit(solution)/shard_map/ppermute | solution.py:22
  29.9 7.5 %collective-permute-start.5 = (bf16[16,2048]{1,0:T(8,128)(2,1)S(1)}, bf16[16,2048]{1,0:T(8,128)(2,1)S(1)}, u32[]{:S(2)}, u32[]{:S(2)}) collective-permute-start(bf16[16,2048]{1,0:T(8,128)(2,1)S(1)} %merge.2), channel_id=1, source_target_pairs={{0,16},{8,24},{16,0},{24,8},{1,17},{9,25},{17,1},{25,9},{2,18},{10... | collective-permute-start | bytes 196616 | tf_op jit(solution)/shard_map/ppermute | solution.py:22
  35.5 4.3 %collective-permute-start.8 = (bf16[16,2048]{1,0:T(8,128)(2,1)S(1)}, bf16[16,2048]{1,0:T(8,128)(2,1)S(1)}, u32[]{:S(2)}, u32[]{:S(2)}) collective-permute-start(bf16[16,2048]{1,0:T(8,128)(2,1)S(1)} %merge.3), channel_id=1, source_target_pairs={{0,16},{8,24},{16,0},{24,8},{1,17},{9,25},{17,1},{25,9},{2,18},{10... | collective-permute-start | bytes 196616 | tf_op jit(solution)/shard_map/ppermute | solution.py:22
  39.9 1.6 %collective-permute-start.9 = (bf16[32,4096]{1,0:T(8,128)(2,1)S(1)}, bf16[32,4096]{1,0:T(8,128)(2,1)S(1)}, u32[]{:S(2)}, u32[]{:S(2)}) collective-permute-start(bf16[32,4096]{1,0:T(8,128)(2,1)S(1)} %pad_maximum_fusion), channel_id=1, source_target_pairs={{0,8},{8,0},{16,24},{24,16},{1,9},{9,1},{17,25},{25,17},{2,10},{10... | collective-permute-start | bytes 786440 | tf_op jit(solution)/shard_map/ppermute | solution.py:22

commit v3 on v2

--- a/solution.py
+++ b/solution.py
@@ -7,10 +7,11 @@
 from jax.experimental.pallas import tpu as pltpu
 from jax.sharding import PartitionSpec as P
 
-CHUNKS = 2
+MIDDLE = 125.0**0.5
+SHIFT = 125.0**0.25
 STEP = 512
 PIECES = 2
-COST = 100
+COST = 10000
 PARAMS = pltpu.CompilerParams(vmem_limit_bytes=16 * 1024 * 1024)
 VMEM = pl.BlockSpec(memory_space=pltpu.VMEM)
 SMEM = pl.BlockSpec(memory_space=pltpu.SMEM)
@@ -152,25 +153,62 @@
     )(block, one, fisher, params, after)
 
 
+def power64(value):
+    for _ in range(6):
+        value = value * value
+    return value
+
+
+def encode(numer, denom, out_ref):
+    cols = numer.shape[1]
+    high = numer.astype(jnp.bfloat16)
+    out_ref[:, :cols] = high
+    out_ref[:, cols : 2 * cols] = (numer - high.astype(jnp.float32)).astype(jnp.bfloat16)
+    top = jnp.full((numer.shape[0], 128), jnp.max(denom), jnp.float32).astype(jnp.bfloat16)
+    out_ref[:, 3 * cols :] = top
+    ratio = denom * (MIDDLE / top[:, :1].astype(jnp.float32))
+    above = ratio >= 1.0
+    code = power64(ratio * jnp.where(above, 1.0 / SHIFT, SHIFT))
+    out_ref[:, 2 * cols : 3 * cols] = jnp.where(above, code, -code).astype(jnp.bfloat16)
+
+
+def decode(ref, rows):
+    cols = (ref.shape[1] - 128) // 3
+    numer = ref[rows, :cols].astype(jnp.float32) + ref[rows, cols : 2 * cols].astype(jnp.float32)
+    code = ref[rows, 2 * cols : 3 * cols].astype(jnp.float32)
+    ratio = jnp.exp2(jnp.log2(jnp.abs(code)) * (1.0 / 64.0)) * jnp.where(code > 0.0, SHIFT, 1.0 / SHIFT)
+    top = ref[rows, 3 * cols : 3 * cols + 1].astype(jnp.float32)
+    return numer, ratio * (top * (1.0 / MIDDLE))
+
+
+def both(one_ref, two_ref, rows):
+    if len(two_ref.shape) == 3:
+        numer, denom = two_ref[0, rows], two_ref[1, rows]
+    else:
+        numer, denom = decode(two_ref, rows)
+    return one_ref[0, rows] + numer, one_ref[1, rows] + denom
+
+
 def split_kernel(upper_ref, one_ref, two_ref, send_ref, keep_ref, token_ref):
     token_ref[0] = upper_ref[0]
-    size = send_ref.shape[1]
+    size = keep_ref.shape[1]
     mine = pl.multiple_of(upper_ref[0] * size, size)
     theirs = pl.multiple_of((1 - upper_ref[0]) * size, size)
-    for k in range(2):
-        send_ref[k] = one_ref[k, pl.ds(theirs, size)] + two_ref[k, pl.ds(theirs, size)]
-        keep_ref[k] = one_ref[k, pl.ds(mine, size)] + two_ref[k, pl.ds(mine, size)]
+    encode(*both(one_ref, two_ref, pl.ds(theirs, size)), send_ref)
+    keep_ref[0], keep_ref[1] = both(one_ref, two_ref, pl.ds(mine, size))
 
 
 def split(upper, one, two):
-    kind = pltpu.VMEM((2, one.shape[1] // 2, one.shape[2]), one.dtype)
-    return pl.pallas_call(
-        split_kernel, in_specs=[SMEM, VMEM, VMEM], out_specs=[VMEM, VMEM, SMEM], out_shape=[kind, kind, pltpu.SMEM((1,), jnp.int32)], compiler_params=PARAMS, name="split"
+    size, cols = one.shape[1] // 2, one.shape[2]
+    kinds = [pltpu.VMEM((size, 3 * cols + 128), jnp.bfloat16), pltpu.VMEM((2, size, cols), one.dtype), pltpu.SMEM((1,), jnp.int32)]
+    return pl.pallas_call(
+        split_kernel, in_specs=[SMEM, VMEM, VMEM], out_specs=[VMEM, VMEM, SMEM], out_shape=kinds, compiler_params=PARAMS, name="split"
     )(upper, one, two)
 
 
 def merge_kernel(one_ref, two_ref, out_ref):
-    out_ref[...] = ((one_ref[0] + two_ref[0]) / (one_ref[1] + two_ref[1])).astype(out_ref.dtype)
+    numer, denom = both(one_ref, two_ref, slice(None))
+    out_ref[...] = (numer / denom).astype(out_ref.dtype)
 
 
 def merge(one, two):
@@ -193,14 +231,14 @@
         one = join(one, swap(one, "param", bit))
     two = swap(one, "param", final)
     first, *rest = bits_of("task")
-    half, cols = rows // 2, width // CHUNKS
+    half, lead = rows // 2, width * 5 // 8
     core = side("task", first)
     uppers = {bit: side("task", bit) for bit in rest}
     after, merged = core, []
     coef = coefs(one, two, count)
-    for chunk in range(CHUNKS):
-        send = weighted(params, fisher, coef, 1 - core, half, chunk * cols, cols, after, "weigh_send")
-        keep = weighted(params, fisher, coef, core, half, chunk * cols, cols, after, "weigh_keep")
+    for col, cols in ((0, lead), (lead, width - lead)):
+        send = weighted(params, fisher, coef, 1 - core, half, col, cols, after, "weigh_send")
+        keep = weighted(params, fisher, coef, core, half, col, cols, after, "weigh_keep")
         other = swap(send, "task", first)
         for bit in rest:
             send, keep, after = split(uppers[bit], keep, other)
@@ -208,9 +246,8 @@
         out = merge(keep, other)
         for bit in reversed(rest):
             out = stacked(uppers[bit], out, swap(out, "task", bit))
-        merged.append(out)
-    out = jnp.concatenate(merged, axis=1)
-    return stacked(core, out, swap(out, "task", first))
+        merged.append(stacked(core, out, swap(out, "task", first)))
+    return jnp.concatenate(merged, axis=1)
 
 
 def solution(mesh):

time: 42.6 us -> 38.4 us (0.901)
  waiting for transfers between devices: 18.1 us -> 12.8 us
  starting transfers between devices: 14.5 us -> 15.1 us
  Pallas kernels: 8.64 us -> 9.16 us
    ppermute x10 -> x11, waiting for transfers between devices: 18.1 us -> 12.8 us  [swap(): return lax.ppermute(value, axis, [(i, i ^ bit) for i in range(size)])]
    concatenate x1, other arithmetic: 0.02 us -> 0.83 us  [local(): return jnp.concatenate(merged, axis=1)]
    select_n x3 -> x4, other arithmetic: 0.93 us -> 0.14 us  [stacked(): jnp.where(upper[0] != 0, jnp.concatenate([other, mine]), jnp.concatenate(...]
    ppermute x10 -> x11, starting transfers between devices: 14.5 us -> 15.1 us  [swap(): return lax.ppermute(value, axis, [(i, i ^ bit) for i in range(size)])]
  transfers between devices with their start and end apart: 10 -> 11, of which waited for: 8 -> 9; matrix products, arithmetic and copies ran while one was open for 0% -> 0% of each run, Pallas kernels for 7% -> 13%
where the time goes in v3:
time: 38.4 us; the launch traced here: 38.2 us
  starting transfers between devices  15.1 us (39%)
  waiting for transfers between devices  12.8 us (33%)
  Pallas kernels  9.16 us (24%)
  other arithmetic  0.97 us (3%)
    ppermute x11, starting transfers between devices, swap(): return lax.ppermute(value, axis, [(i, i ^ bit) for i in range(size)])  15.1 us
    ppermute x11, waiting for transfers between devices, swap(): return lax.ppermute(value, axis, [(i, i ^ bit) for i in range(size)])  12.8 us
    pallas_call x4, Pallas kernels, weighted(): pl.pallas_call(functools.partial(weigh_kernel, col=col), in_specs=[SMEM,...  6.03 us
    pallas_call x1, Pallas kernels, local_stats(): pl.pallas_call(stats_kernel, in_specs=[HBM], out_specs=VMEM, out_shape=pl...  2.37 us
    concatenate x1, other arithmetic, local(): return jnp.concatenate(merged, axis=1)  0.83 us
  transfers between devices with their start and end apart: 11, of which 9 were waited for; matrix products, arithmetic and copies ran while one was open for 0% of the time, Pallas kernels for 13%

profile of v3, /device:TPU:0, one launch (start us, length us, event | category | flops | bytes accessed | tf_op | source)
XLA Modules:
  0.0 38.2 jit_solution(2381252080863055742)
XLA Ops:
  0.0 2.4 %local_stats.1.one_ref = f32[8,128]{1,0:T(8,128)S(1)} custom-call(f32[4,64,4096]{2,1,0:T(8,128)} %fisher_hbm.7), custom_call_target="tpu_custom_call" | custom-call | tf_op jit(solution)/shard_map/local_stats/pallas_call | solution.py:60
  2.4 3.0 %collective-permute-start = (f32[8,128]{1,0:T(8,128)S(1)}, f32[8,128]{1,0:T(8,128)S(1)}, u32[]{:S(2)}, u32[]{:S(2)}) collective-permute-start(f32[8,128]{1,0:T(8,128)S(1)} %local_stats.1.one_ref), channel_id=1, source_target_pairs={{0,1},{1,0},{2,3},{3,2},{4,5},{5,4},{6,7},{7,6},{8,9},{9,8},{10,11... | collective-permute-start | bytes 12296 | tf_op jit(solution)/shard_map/ppermute | solution.py:23
  5.4 1.6 %collective-permute-done.two_ref = f32[8,128]{1,0:T(8,128)S(1)} collective-permute-done((f32[8,128]{1,0:T(8,128)S(1)}, f32[8,128]{1,0:T(8,128)S(1)}, u32[]{:S(2)}, u32[]{:S(2)}) %collective-permute-start) | collective-permute-done | bytes 4128 | tf_op jit(solution)/shard_map/ppermute | solution.py:23
  7.0 2.1 %collective-permute-start.1 = (f32[8,128]{1,0:T(8,128)S(1)}, f32[8,128]{1,0:T(8,128)S(1)}, u32[]{:S(2)}, u32[]{:S(2)}) collective-permute-start(f32[8,128]{1,0:T(8,128)S(1)} %join.2.one_ref), channel_id=1, source_target_pairs={{0,2},{1,3},{2,0},{3,1},{4,6},{5,7},{6,4},{7,5},{8,10},{9,11},{10,... | collective-permute-start | bytes 12296 | tf_op jit(solution)/shard_map/ppermute | solution.py:23
  9.1 1.6 %collective-permute-done.1.two_ref = f32[8,128]{1,0:T(8,128)S(1)} collective-permute-done((f32[8,128]{1,0:T(8,128)S(1)}, f32[8,128]{1,0:T(8,128)S(1)}, u32[]{:S(2)}, u32[]{:S(2)}) %collective-permute-start.1) | collective-permute-done | bytes 4128 | tf_op jit(solution)/shard_map/ppermute | solution.py:23
  10.7 3.0 %collective-permute-start.2 = (f32[8,128]{1,0:T(8,128)S(1)}, f32[8,128]{1,0:T(8,128)S(1)}, u32[]{:S(2)}, u32[]{:S(2)}) collective-permute-start(f32[8,128]{1,0:T(8,128)S(1)} %join.3.one_ref), channel_id=1, source_target_pairs={{0,4},{1,5},{2,6},{3,7},{4,0},{5,1},{6,2},{7,3},{8,12},{9,13},{10,... | collective-permute-start | bytes 12296 | tf_op jit(solution)/shard_map/ppermute | solution.py:23
  13.7 1.6 %collective-permute-done.2.two_ref = f32[8,128]{1,0:T(8,128)S(1)} collective-permute-done((f32[8,128]{1,0:T(8,128)S(1)}, f32[8,128]{1,0:T(8,128)S(1)}, u32[]{:S(2)}, u32[]{:S(2)}) %collective-permute-start.2) | collective-permute-done | bytes 4128 | tf_op jit(solution)/shard_map/ppermute | solution.py:23
  15.4 1.7 %weigh_send.2 = f32[2,32,2560]{2,1,0:T(8,128)S(1)} custom-call(s32[1]{0:T(128)S(6)} %sub.4.half_ref, f32[12,1]{1,0:T(8,128)S(4)} %coefs.1.stats_ref, f32[4,64,4096]{2,1,0:T(8,128)} %fisher_hbm.7, bf16[4,64,4096]{2,1,0:T(8,128)(2,1)} %params_hbm.7, s32[1]{0:T(128)} %bitcast.1.half_ref.after_ref), custom_call_target="tpu_custom_call" | custom-call | flops 26214400000 | bytes 1966080 | tf_op jit(solution)/shard_map/weigh_send/pallas_call | solution.py:141
  17.1 1.7 %weigh_keep.2.one_ref = f32[2,32,2560]{2,1,0:T(8,128)S(1)} custom-call(s32[1]{0:T(128)} %bitcast.1.half_ref.after_ref, f32[12,1]{1,0:T(8,128)S(4)} %coefs.1.stats_ref, f32[4,64,4096]{2,1,0:T(8,128)} %fisher_hbm.7, bf16[4,64,4096]{2,1,0:T(8,128)(2,1)} %params_hbm.7, s32[1]{0:T(128)} %bitcast.1.half_ref.after_ref), custom_call_target="tpu_custom_call" | custom-call | flops 26214400000 | bytes 1966080 | tf_op jit(solution)/shard_map/weigh_keep/pallas_call | solution.py:141
  18.8 0.4 %collective-permute-done.3.two_ref = f32[2,32,2560]{2,1,0:T(8,128)S(1)} collective-permute-done((f32[2,32,2560]{2,1,0:T(8,128)S(1)}, f32[2,32,2560]{2,1,0:T(8,128)S(1)}, u32[]{:S(2)}, u32[]{:S(2)}) %collective-permute-start.3) | collective-permute-done | bytes 655392 | tf_op jit(solution)/shard_map/ppermute | solution.py:23
  19.2 0.3 split.2
  19.5 1.9 %collective-permute-start.4 = (bf16[16,7808]{1,0:T(8,128)(2,1)S(1)}, bf16[16,7808]{1,0:T(8,128)(2,1)S(1)}, u32[]{:S(2)}, u32[]{:S(2)}) collective-permute-start(bf16[16,7808]{1,0:T(8,128)(2,1)S(1)} %get-tuple-element.11), channel_id=1, source_target_pairs={{0,16},{8,24},{16,0},{24,8},{1,17},{9,25},{17,1},{25,9},{2,18},{10... | collective-permute-start | bytes 749576 | tf_op jit(solution)/shard_map/ppermute | solution.py:23
  21.4 1.4 %weigh_send.3 = f32[2,32,1536]{2,1,0:T(8,128)S(1)} custom-call(s32[1]{0:T(128)S(6)} %sub.4.half_ref, f32[12,1]{1,0:T(8,128)S(4)} %coefs.1.stats_ref, f32[4,64,4096]{2,1,0:T(8,128)} %fisher_hbm.7, bf16[4,64,4096]{2,1,0:T(8,128)(2,1)} %params_hbm.7, s32[1]{0:T(128)S(4)} %get-tuple-element.12.after_ref), custom_call_target="tpu_custom_call" | custom-call | flops 15728640000 | bytes 1179648 | tf_op jit(solution)/shard_map/weigh_send/pallas_call | solution.py:141
  22.9 1.4 %weigh_keep.3.one_ref = f32[2,32,1536]{2,1,0:T(8,128)S(1)} custom-call(s32[1]{0:T(128)} %bitcast.1.half_ref.after_ref, f32[12,1]{1,0:T(8,128)S(4)} %coefs.1.stats_ref, f32[4,64,4096]{2,1,0:T(8,128)} %fisher_hbm.7, bf16[4,64,4096]{2,1,0:T(8,128)(2,1)} %params_hbm.7, s32[1]{0:T(128)S(4)} %get-tuple-element.12.after_ref), custom_call_target="tpu_custom_call" | custom-call | flops 15728640000 | bytes 1179648 | tf_op jit(solution)/shard_map/weigh_keep/pallas_call | solution.py:141
  24.2 0.3 collective-permute-done.7.two_ref
  24.6 0.2 split.3
  24.8 0.2 collective-permute-start.8
  25.0 2.9 %collective-permute-done.4.two_ref = bf16[16,7808]{1,0:T(8,128)(2,1)S(1)} collective-permute-done((bf16[16,7808]{1,0:T(8,128)(2,1)S(1)}, bf16[16,7808]{1,0:T(8,128)(2,1)S(1)}, u32[]{:S(2)}, u32[]{:S(2)}) %collective-permute-start.4) | collective-permute-done | bytes 249888 | tf_op jit(solution)/shard_map/ppermute | solution.py:23
  28.0 2.5 %collective-permute-start.5 = (bf16[16,2560]{1,0:T(8,128)(2,1)S(1)}, bf16[16,2560]{1,0:T(8,128)(2,1)S(1)}, u32[]{:S(2)}, u32[]{:S(2)}) collective-permute-start(bf16[16,2560]{1,0:T(8,128)(2,1)S(1)} %merge.2), channel_id=1, source_target_pairs={{0,16},{8,24},{16,0},{24,8},{1,17},{9,25},{17,1},{25,9},{2,18},{10... | collective-permute-start | bytes 245768 | tf_op jit(solution)/shard_map/ppermute | solution.py:23
  30.5 1.1 %collective-permute-done.8.two_ref = bf16[16,4736]{1,0:T(8,128)(2,1)S(1)} collective-permute-done((bf16[16,4736]{1,0:T(8,128)(2,1)S(1)}, bf16[16,4736]{1,0:T(8,128)(2,1)S(1)}, u32[]{:S(2)}, u32[]{:S(2)}) %collective-permute-start.8) | collective-permute-done | bytes 151584 | tf_op jit(solution)/shard_map/ppermute | solution.py:23
  31.8 2.0 %collective-permute-start.9 = (bf16[16,1536]{1,0:T(8,128)(2,1)S(1)}, bf16[16,1536]{1,0:T(8,128)(2,1)S(1)}, u32[]{:S(2)}, u32[]{:S(2)}) collective-permute-start(bf16[16,1536]{1,0:T(8,128)(2,1)S(1)} %merge.3), channel_id=1, source_target_pairs={{0,16},{8,24},{16,0},{24,8},{1,17},{9,25},{17,1},{25,9},{2,18},{10... | collective-permute-start | bytes 147464 | tf_op jit(solution)/shard_map/ppermute | solution.py:23
  33.9 2.0 %collective-permute-done.9 = bf16[16,1536]{1,0:T(8,128)(2,1)S(1)} collective-permute-done((bf16[16,1536]{1,0:T(8,128)(2,1)S(1)}, bf16[16,1536]{1,0:T(8,128)(2,1)S(1)}, u32[]{:S(2)}, u32[]{:S(2)}) %collective-permute-start.9) | collective-permute-done | bytes 49184 | tf_op jit(solution)/shard_map/ppermute | solution.py:23
  36.1 1.2 %collective-permute-done.10 = bf16[32,1536]{1,0:T(8,128)(2,1)S(1)} collective-permute-done((bf16[32,1536]{1,0:T(8,128)(2,1)S(1)}, bf16[32,1536]{1,0:T(8,128)(2,1)S(1)}, u32[]{:S(2)}, u32[]{:S(2)}) %collective-permute-start.10) | collective-permute-done | bytes 98336 | tf_op jit(solution)/shard_map/ppermute | solution.py:23
  37.3 0.8 %pad_maximum_fusion = bf16[64,4096]{1,0:T(8,128)(2,1)} fusion(bf16[64,1536]{1,0:T(8,128)(2,1)S(1)} %maximum_select_fusion.1, bf16[64,2560]{1,0:T(8,128)(2,1)S(1)} %maximum_select_fusion), kind=kLoop, calls=%fused_computation | loop fusion | flops 1048576 | bytes 1048576 | tf_op jit(solution)/shard_map/concatenate | solution.py:250
  (15 shorter events, 0.7 us)
Async XLA Ops:
  2.4 4.6 %collective-permute-start = (f32[8,128]{1,0:T(8,128)S(1)}, f32[8,128]{1,0:T(8,128)S(1)}, u32[]{:S(2)}, u32[]{:S(2)}) collective-permute-start(f32[8,128]{1,0:T(8,128)S(1)} %local_stats.1.one_ref), channel_id=1, source_target_pairs={{0,1},{1,0},{2,3},{3,2},{4,5},{5,4},{6,7},{7,6},{8,9},{9,8},{10,11... | collective-permute-start | bytes 12296 | tf_op jit(solution)/shard_map/ppermute | solution.py:23
  7.0 3.7 %collective-permute-start.1 = (f32[8,128]{1,0:T(8,128)S(1)}, f32[8,128]{1,0:T(8,128)S(1)}, u32[]{:S(2)}, u32[]{:S(2)}) collective-permute-start(f32[8,128]{1,0:T(8,128)S(1)} %join.2.one_ref), channel_id=1, source_target_pairs={{0,2},{1,3},{2,0},{3,1},{4,6},{5,7},{6,4},{7,5},{8,10},{9,11},{10,... | collective-permute-start | bytes 12296 | tf_op jit(solution)/shard_map/ppermute | solution.py:23
  10.7 4.6 %collective-permute-start.2 = (f32[8,128]{1,0:T(8,128)S(1)}, f32[8,128]{1,0:T(8,128)S(1)}, u32[]{:S(2)}, u32[]{:S(2)}) collective-permute-start(f32[8,128]{1,0:T(8,128)S(1)} %join.3.one_ref), channel_id=1, source_target_pairs={{0,4},{1,5},{2,6},{3,7},{4,0},{5,1},{6,2},{7,3},{8,12},{9,13},{10,... | collective-permute-start | bytes 12296 | tf_op jit(solution)/shard_map/ppermute | solution.py:23
  17.0 2.2 %collective-permute-start.3 = (f32[2,32,2560]{2,1,0:T(8,128)S(1)}, f32[2,32,2560]{2,1,0:T(8,128)S(1)}, u32[]{:S(2)}, u32[]{:S(2)}) collective-permute-start(f32[2,32,2560]{2,1,0:T(8,128)S(1)} %weigh_send.2), channel_id=1, source_target_pairs={{0,8},{8,0},{16,24},{24,16},{1,9},{9,1},{17,25},{25,17},{2,10},{10... | collective-permute-start | bytes 1966088 | tf_op jit(solution)/shard_map/ppermute | solution.py:23
  19.5 8.4 %collective-permute-start.4 = (bf16[16,7808]{1,0:T(8,128)(2,1)S(1)}, bf16[16,7808]{1,0:T(8,128)(2,1)S(1)}, u32[]{:S(2)}, u32[]{:S(2)}) collective-permute-start(bf16[16,7808]{1,0:T(8,128)(2,1)S(1)} %get-tuple-element.11), channel_id=1, source_target_pairs={{0,16},{8,24},{16,0},{24,8},{1,17},{9,25},{17,1},{25,9},{2,18},{10... | collective-permute-start | bytes 749576 | tf_op jit(solution)/shard_map/ppermute | solution.py:23
  22.8 1.8 %collective-permute-start.7 = (f32[2,32,1536]{2,1,0:T(8,128)S(1)}, f32[2,32,1536]{2,1,0:T(8,128)S(1)}, u32[]{:S(2)}, u32[]{:S(2)}) collective-permute-start(f32[2,32,1536]{2,1,0:T(8,128)S(1)} %weigh_send.3), channel_id=1, source_target_pairs={{0,8},{8,0},{16,24},{24,16},{1,9},{9,1},{17,25},{25,17},{2,10},{10... | collective-permute-start | bytes 1179656 | tf_op jit(solution)/shard_map/ppermute | solution.py:23
  24.8 6.9 %collective-permute-start.8 = (bf16[16,4736]{1,0:T(8,128)(2,1)S(1)}, bf16[16,4736]{1,0:T(8,128)(2,1)S(1)}, u32[]{:S(2)}, u32[]{:S(2)}) collective-permute-start(bf16[16,4736]{1,0:T(8,128)(2,1)S(1)} %get-tuple-element.14), channel_id=1, source_target_pairs={{0,16},{8,24},{16,0},{24,8},{1,17},{9,25},{17,1},{25,9},{2,18},{10... | collective-permute-start | bytes 454664 | tf_op jit(solution)/shard_map/ppermute | solution.py:23
  28.0 5.7 %collective-permute-start.5 = (bf16[16,2560]{1,0:T(8,128)(2,1)S(1)}, bf16[16,2560]{1,0:T(8,128)(2,1)S(1)}, u32[]{:S(2)}, u32[]{:S(2)}) collective-permute-start(bf16[16,2560]{1,0:T(8,128)(2,1)S(1)} %merge.2), channel_id=1, source_target_pairs={{0,16},{8,24},{16,0},{24,8},{1,17},{9,25},{17,1},{25,9},{2,18},{10... | collective-permute-start | bytes 245768 | tf_op jit(solution)/shard_map/ppermute | solution.py:23
  31.8 4.2 %collective-permute-start.9 = (bf16[16,1536]{1,0:T(8,128)(2,1)S(1)}, bf16[16,1536]{1,0:T(8,128)(2,1)S(1)}, u32[]{:S(2)}, u32[]{:S(2)}) collective-permute-start(bf16[16,1536]{1,0:T(8,128)(2,1)S(1)} %merge.3), channel_id=1, source_target_pairs={{0,16},{8,24},{16,0},{24,8},{1,17},{9,25},{17,1},{25,9},{2,18},{10... | collective-permute-start | bytes 147464 | tf_op jit(solution)/shard_map/ppermute | solution.py:23
  33.8 2.2 %collective-permute-start.6 = (bf16[32,2560]{1,0:T(8,128)(2,1)S(1)}, bf16[32,2560]{1,0:T(8,128)(2,1)S(1)}, u32[]{:S(2)}, u32[]{:S(2)}) collective-permute-start(bf16[32,2560]{1,0:T(8,128)(2,1)S(1)} %maximum_select_fusion.2), channel_id=1, source_target_pairs={{0,8},{8,0},{16,24},{24,16},{1,9},{9,1},{17,25},{25,17},{2,10},{10... | collective-permute-start | bytes 491528 | tf_op jit(solution)/shard_map/ppermute | solution.py:23
  35.9 1.4 %collective-permute-start.10 = (bf16[32,1536]{1,0:T(8,128)(2,1)S(1)}, bf16[32,1536]{1,0:T(8,128)(2,1)S(1)}, u32[]{:S(2)}, u32[]{:S(2)}) collective-permute-start(bf16[32,1536]{1,0:T(8,128)(2,1)S(1)} %maximum_select_fusion.3), channel_id=1, source_target_pairs={{0,8},{8,0},{16,24},{24,16},{1,9},{9,1},{17,25},{25,17},{2,10},{10... | collective-permute-start | bytes 294920 | tf_op jit(solution)/shard_map/ppermute | solution.py:23

commit v4 on v3

--- a/solution.py
+++ b/solution.py
@@ -1,4 +1,5 @@
 import functools
+import math
 
 import jax
 import jax.numpy as jnp
@@ -12,6 +13,8 @@
 STEP = 512
 PIECES = 2
 COST = 10000
+FETCH_COST = 10000
+FETCHED_COST = 10000
 PARAMS = pltpu.CompilerParams(vmem_limit_bytes=16 * 1024 * 1024)
 VMEM = pl.BlockSpec(memory_space=pltpu.VMEM)
 SMEM = pl.BlockSpec(memory_space=pltpu.SMEM)
@@ -73,36 +76,110 @@
     return jnp.maximum(one[:tasks], two[:tasks]), one[tasks:] + two[tasks:]
 
 
-def join_kernel(one_ref, two_ref, out_ref):
+def join_kernel(one_ref, two_ref, out_ref, scalars_ref):
     tasks = one_ref.shape[0] // 2
-    out_ref[:tasks], out_ref[tasks:] = joined(one_ref, two_ref)
+    peak, total = joined(one_ref, two_ref)
+    out_ref[:tasks], out_ref[tasks:] = peak, total
+    for task in range(tasks):
+        scalars_ref[task, 0] = peak[task, 0]
+        scalars_ref[tasks + task, 0] = total[task, 0]
 
 
 def join(one, two):
     return pl.pallas_call(
-        join_kernel, in_specs=[VMEM] * 2, out_specs=VMEM, out_shape=pltpu.VMEM(one.shape, one.dtype), compiler_params=PARAMS, name="join"
+        join_kernel,
+        in_specs=[VMEM] * 2,
+        out_specs=[VMEM, SMEM],
+        out_shape=[pltpu.VMEM(one.shape, one.dtype), pltpu.SMEM((one.shape[0], 1), one.dtype)],
+        compiler_params=PARAMS,
+        name="join",
     )(one, two)
 
 
-def coef_kernel(one_ref, two_ref, out_ref, *, count):
-    peak, total = joined(one_ref, two_ref)
-    scale = count / total
-    factor = scale * peak
-    for k, value in enumerate([scale, 0.002 * factor, 0.25 * factor]):
-        for task in range(value.shape[0]):
-            out_ref[k * value.shape[0] + task, 0] = value[task, 0]
-
-
-def coefs(one, two, count):
-    kind = pltpu.SMEM((3 * one.shape[0] // 2, 1), jnp.float32)
+def coef_kernel(scalars_ref, two_ref, out_ref, *, count):
+    tasks = two_ref.shape[0] // 2
+    for task in range(tasks):
+        peak = jnp.maximum(two_ref[task : task + 1], scalars_ref[task, 0])
+        total = two_ref[tasks + task : tasks + task + 1] + scalars_ref[tasks + task, 0]
+        scale = count / total
+        factor = scale * peak
+        for k, value in enumerate([scale, 0.002 * factor, 0.25 * factor]):
+            out_ref[k * tasks + task, 0] = value[0, 0]
+
+
+def coefs(scalars, two, count):
+    kind = pltpu.SMEM((3 * two.shape[0] // 2, 1), jnp.float32)
     return pl.pallas_call(
         functools.partial(coef_kernel, count=count),
-        in_specs=[VMEM] * 2,
+        in_specs=[SMEM, VMEM],
         out_specs=SMEM,
         out_shape=kind,
         compiler_params=PARAMS,
         name="coefs",
-    )(one, two)
+    )(scalars, two)
+
+
+def fetch_kernel(half_ref, after_ref, fisher_hbm, params_hbm, fisher_ref, params_ref, sems, *, col):
+    tasks, rows, cols = fisher_ref.shape
+    start = pl.ds(pl.multiple_of(half_ref[0] * rows, rows), rows)
+    copies = [
+        pltpu.make_async_copy(hbm.at[:, start, pl.ds(col, cols)], ref, sems.at[k])
+        for k, (hbm, ref) in enumerate([(fisher_hbm, fisher_ref), (params_hbm, params_ref)])
+    ]
+    for copy in copies:
+        copy.start()
+    for copy in copies:
+        copy.wait()
+
+
+def fetch(params, fisher, after, block, rows, col, cols):
+    shape = (fisher.shape[0], rows, cols)
+    return pl.pallas_call(
+        functools.partial(fetch_kernel, col=col),
+        in_specs=[SMEM, SMEM, HBM, HBM],
+        out_specs=[VMEM] * 2,
+        out_shape=[pltpu.VMEM(shape, jnp.float32), pltpu.VMEM(shape, jnp.bfloat16)],
+        scratch_shapes=[pltpu.SemaphoreType.DMA((2,))],
+        cost_estimate=pl.CostEstimate(flops=8 * math.prod(shape) * FETCH_COST, transcendentals=0, bytes_accessed=6 * math.prod(shape)),
+        name="fetch",
+    )(block, after, fisher, params)
+
+
+def weigh_fetched_kernel(stats_ref, fisher_ref, params_ref, out_ref):
+    rows, cols = fisher_ref.shape[1:]
+    coef = coef_of(stats_ref, fisher_ref.shape[0])
+    for col in range(0, cols, STEP):
+        weigh(coef, fisher_ref, params_ref, out_ref, col, min(STEP, cols - col))
+
+
+def weighted_fetched(params, fisher, coef, name):
+    tasks, rows, cols = fisher.shape
+    return pl.pallas_call(
+        weigh_fetched_kernel,
+        in_specs=[SMEM, VMEM, VMEM],
+        out_specs=VMEM,
+        out_shape=pltpu.VMEM((2, rows, cols), jnp.float32),
+        cost_estimate=pl.CostEstimate(flops=8 * tasks * rows * cols * FETCHED_COST, transcendentals=0, bytes_accessed=6 * tasks * rows * cols),
+        compiler_params=PARAMS,
+        name=name,
+    )(coef, fisher, params)
+
+
+def coef_of(stats_ref, tasks):
+    return [tuple(stats_ref[k * tasks + task, 0] for k in range(3)) for task in range(tasks)]
+
+
+def weigh(coef, fisher_ref, params_ref, out_ref, col, step):
+    for row in range(0, out_ref.shape[1], 8):
+        place = (slice(row, row + 8), slice(col, col + step))
+        numer = denom = None
+        for task, (by, least, most) in enumerate(coef):
+            weight = jnp.minimum(jnp.maximum(fisher_ref[(task,) + place] * by, least), most)
+            term = weight * params_ref[(task,) + place].astype(jnp.float32)
+            numer = term if task == 0 else numer + term
+            denom = weight if task == 0 else denom + weight
+        out_ref[(0,) + place] = numer
+        out_ref[(1,) + place] = denom
 
 
 def weigh_kernel(half_ref, stats_ref, fisher_hbm, params_hbm, after_ref, out_ref, fisher_ref, params_ref, sems, *, col):
@@ -119,21 +196,11 @@
         for copy in pair:
             copy.start()
         loads.append(pair)
-    coef = [tuple(stats_ref[k * tasks + task, 0] for k in range(3)) for task in range(tasks)]
+    coef = coef_of(stats_ref, tasks)
     for piece in range(cols // step):
         for copy in loads[piece]:
             copy.wait()
-        for row in range(0, rows, 8):
-            place = (slice(row, row + 8), slice(piece * step, piece * step + step))
-            numer = denom = None
-            for task in range(tasks):
-                by, least, most = coef[task]
-                weight = jnp.minimum(jnp.maximum(fisher_ref[(task,) + place] * by, least), most)
-                term = weight * params_ref[(task,) + place].astype(jnp.float32)
-                numer = term if task == 0 else numer + term
-                denom = weight if task == 0 else denom + weight
-            out_ref[(0,) + place] = numer
-            out_ref[(1,) + place] = denom
+        weigh(coef, fisher_ref, params_ref, out_ref, piece * step, step)
 
 
 def weighted(params, fisher, one, block, rows, col, cols, after, name):
@@ -228,16 +295,20 @@
     one = local_stats(fisher)
     *early, final = bits_of("param")
     for bit in early:
-        one = join(one, swap(one, "param", bit))
-    two = swap(one, "param", final)
+        one, scalars = join(one, swap(one, "param", bit))
     first, *rest = bits_of("task")
     half, lead = rows // 2, width * 5 // 8
     core = side("task", first)
     uppers = {bit: side("task", bit) for bit in rest}
-    after, merged = core, []
-    coef = coefs(one, two, count)
+    two = swap(one, "param", final)
+    fetched = fetch(params, fisher, scalars, 1 - core, half, 0, lead)
+    coef = coefs(scalars, two, count)
+    after, whole = core, []
     for col, cols in ((0, lead), (lead, width - lead)):
-        send = weighted(params, fisher, coef, 1 - core, half, col, cols, after, "weigh_send")
+        if col == 0:
+            send = weighted_fetched(fetched[1], fetched[0], coef, "weigh_fetched")
+        else:
+            send = weighted(params, fisher, coef, 1 - core, half, col, cols, after, "weigh_send")
         keep = weighted(params, fisher, coef, core, half, col, cols, after, "weigh_keep")
         other = swap(send, "task", first)
         for bit in rest:
@@ -246,8 +317,9 @@
         out = merge(keep, other)
         for bit in reversed(rest):
             out = stacked(uppers[bit], out, swap(out, "task", bit))
-        merged.append(stacked(core, out, swap(out, "task", first)))
-    return jnp.concatenate(merged, axis=1)
+        part = stacked(core, out, swap(out, "task", first))
+        whole.append(part)
+    return jnp.concatenate(whole, axis=1)
 
 
 def solution(mesh):

time: 38.4 us -> 37.3 us (0.971)
  waiting for transfers between devices: 12.8 us -> 11.3 us
    pallas_call x3 -> x5, Pallas kernels: 0.06 us -> 1.93 us  [the longest x1 1.5 us: fetch(): pl.pallas_call(functools.partial(fetch_kernel, col=col), in_specs=[SMEM,...]
    pallas_call x4 -> x3, Pallas kernels: 6.03 us -> 4.38 us  [weighted(): pl.pallas_call(functools.partial(weigh_kernel, col=col), in_specs=[SMEM,...]
    ppermute x11, waiting for transfers between devices: 12.8 us -> 11.3 us  [swap(): return lax.ppermute(value, axis, [(i, i ^ bit) for i in range(size)])]
  transfers between devices with their start and end apart: 11 -> 11, of which waited for: 9 -> 9; matrix products, arithmetic and copies ran while one was open for 0% -> 0% of each run, Pallas kernels for 13% -> 17%
where the time goes in v4:
time: 37.3 us; the launch traced here: 37 us
  starting transfers between devices  15.2 us (41%)
  waiting for transfers between devices  11.3 us (30%)
  Pallas kernels  9.38 us (25%)
  other arithmetic  0.97 us (3%)
    ppermute x11, starting transfers between devices, swap(): return lax.ppermute(value, axis, [(i, i ^ bit) for i in range(size)])  15.2 us
    ppermute x11, waiting for transfers between devices, swap(): return lax.ppermute(value, axis, [(i, i ^ bit) for i in range(size)])  11.3 us
    pallas_call x3, Pallas kernels, weighted(): pl.pallas_call(functools.partial(weigh_kernel, col=col), in_specs=[SMEM,...  4.38 us
    pallas_call x1, Pallas kernels, local_stats(): pl.pallas_call(stats_kernel, in_specs=[HBM], out_specs=VMEM, out_shape=pl...  2.37 us
    pallas_call x1, Pallas kernels, fetch(): pl.pallas_call(functools.partial(fetch_kernel, col=col), in_specs=[SMEM,...  1.5 us
    concatenate x1, other arithmetic, local(): return jnp.concatenate(whole, axis=1)  0.83 us
  transfers between devices with their start and end apart: 11, of which 9 were waited for; matrix products, arithmetic and copies ran while one was open for 0% of the time, Pallas kernels for 17%

profile of v4, /device:TPU:0, one launch (start us, length us, event | category | flops | bytes accessed | tf_op | source)
XLA Modules:
  0.0 37.0 jit_solution(12800409136441403850)
XLA Ops:
  0.0 2.4 %local_stats.1.one_ref = f32[8,128]{1,0:T(8,128)S(1)} custom-call(f32[4,64,4096]{2,1,0:T(8,128)} %fisher_hbm.7), custom_call_target="tpu_custom_call" | custom-call | tf_op jit(solution)/shard_map/local_stats/pallas_call | solution.py:63
  2.4 3.0 %collective-permute-start = (f32[8,128]{1,0:T(8,128)S(1)}, f32[8,128]{1,0:T(8,128)S(1)}, u32[]{:S(2)}, u32[]{:S(2)}) collective-permute-start(f32[8,128]{1,0:T(8,128)S(1)} %local_stats.1.one_ref), channel_id=1, source_target_pairs={{0,1},{1,0},{2,3},{3,2},{4,5},{5,4},{6,7},{7,6},{8,9},{9,8},{10,11... | collective-permute-start | bytes 12296 | tf_op jit(solution)/shard_map/ppermute | solution.py:26
  5.4 1.6 %collective-permute-done.two_ref = f32[8,128]{1,0:T(8,128)S(1)} collective-permute-done((f32[8,128]{1,0:T(8,128)S(1)}, f32[8,128]{1,0:T(8,128)S(1)}, u32[]{:S(2)}, u32[]{:S(2)}) %collective-permute-start) | collective-permute-done | bytes 4128 | tf_op jit(solution)/shard_map/ppermute | solution.py:26
  7.1 2.2 %collective-permute-start.1 = (f32[8,128]{1,0:T(8,128)S(1)}, f32[8,128]{1,0:T(8,128)S(1)}, u32[]{:S(2)}, u32[]{:S(2)}) collective-permute-start(f32[8,128]{1,0:T(8,128)S(1)} %get-tuple-element.15.one_ref), channel_id=1, source_target_pairs={{0,2},{1,3},{2,0},{3,1},{4,6},{5,7},{6,4},{7,5},{8,10},{9,11},{10,... | collective-permute-start | bytes 12296 | tf_op jit(solution)/shard_map/ppermute | solution.py:26
  9.2 1.6 %collective-permute-done.1.two_ref = f32[8,128]{1,0:T(8,128)S(1)} collective-permute-done((f32[8,128]{1,0:T(8,128)S(1)}, f32[8,128]{1,0:T(8,128)S(1)}, u32[]{:S(2)}, u32[]{:S(2)}) %collective-permute-start.1) | collective-permute-done | bytes 4128 | tf_op jit(solution)/shard_map/ppermute | solution.py:26
  10.9 3.1 %collective-permute-start.2 = (f32[8,128]{1,0:T(8,128)S(1)}, f32[8,128]{1,0:T(8,128)S(1)}, u32[]{:S(2)}, u32[]{:S(2)}) collective-permute-start(f32[8,128]{1,0:T(8,128)S(1)} %get-tuple-element.17), channel_id=1, source_target_pairs={{0,4},{1,5},{2,6},{3,7},{4,0},{5,1},{6,2},{7,3},{8,12},{9,13},{10,... | collective-permute-start | bytes 12296 | tf_op jit(solution)/shard_map/ppermute | solution.py:26
  14.0 1.5 %fetch.1 = (f32[4,32,2560]{2,1,0:T(8,128)S(1)}, bf16[4,32,2560]{2,1,0:T(8,128)(2,1)S(1)}) custom-call(s32[1]{0:T(128)S(6)} %sub.4.half_ref, f32[8,1]{1,0:T(8,128)S(4)} %get-tuple-element.16.scalars_ref.after_ref, f32[4,64,4096]{2,1,0:T(8,128)} %fisher_hbm.7, bf16[4,64,4096]{2,1,0:T(8,128)(2,1)} %params_hbm.7), custom_call_target="tpu_custom_call" | custom-call | flops 26214400000 | bytes 1966080 | tf_op jit(solution)/shard_map/fetch/pallas_call | solution.py:137
  15.6 0.3 weigh_fetched.1
  16.0 1.7 %weigh_keep.2.one_ref = f32[2,32,2560]{2,1,0:T(8,128)S(1)} custom-call(s32[1]{0:T(128)} %bitcast.1.half_ref.after_ref, f32[12,1]{1,0:T(8,128)S(4)} %coefs.1.stats_ref, f32[4,64,4096]{2,1,0:T(8,128)} %fisher_hbm.7, bf16[4,64,4096]{2,1,0:T(8,128)(2,1)} %params_hbm.7, s32[1]{0:T(128)} %bitcast.1.half_ref.after_ref), custom_call_target="tpu_custom_call" | custom-call | flops 26214400000 | bytes 1966080 | tf_op jit(solution)/shard_map/weigh_keep/pallas_call | solution.py:208
  17.6 0.4 %collective-permute-done.3.two_ref = f32[2,32,2560]{2,1,0:T(8,128)S(1)} collective-permute-done((f32[2,32,2560]{2,1,0:T(8,128)S(1)}, f32[2,32,2560]{2,1,0:T(8,128)S(1)}, u32[]{:S(2)}, u32[]{:S(2)}) %collective-permute-start.3) | collective-permute-done | bytes 655392 | tf_op jit(solution)/shard_map/ppermute | solution.py:26
  18.1 0.3 split.2
  18.4 1.9 %collective-permute-start.4 = (bf16[16,7808]{1,0:T(8,128)(2,1)S(1)}, bf16[16,7808]{1,0:T(8,128)(2,1)S(1)}, u32[]{:S(2)}, u32[]{:S(2)}) collective-permute-start(bf16[16,7808]{1,0:T(8,128)(2,1)S(1)} %get-tuple-element.21), channel_id=1, source_target_pairs={{0,16},{8,24},{16,0},{24,8},{1,17},{9,25},{17,1},{25,9},{2,18},{10... | collective-permute-start | bytes 749576 | tf_op jit(solution)/shard_map/ppermute | solution.py:26
  20.3 1.4 %weigh_send.1 = f32[2,32,1536]{2,1,0:T(8,128)S(1)} custom-call(s32[1]{0:T(128)S(6)} %sub.4.half_ref, f32[12,1]{1,0:T(8,128)S(4)} %coefs.1.stats_ref, f32[4,64,4096]{2,1,0:T(8,128)} %fisher_hbm.7, bf16[4,64,4096]{2,1,0:T(8,128)(2,1)} %params_hbm.7, s32[1]{0:T(128)S(4)} %get-tuple-element.22.after_ref), custom_call_target="tpu_custom_call" | custom-call | flops 15728640000 | bytes 1179648 | tf_op jit(solution)/shard_map/weigh_send/pallas_call | solution.py:208
  21.7 1.4 %weigh_keep.3.one_ref = f32[2,32,1536]{2,1,0:T(8,128)S(1)} custom-call(s32[1]{0:T(128)} %bitcast.1.half_ref.after_ref, f32[12,1]{1,0:T(8,128)S(4)} %coefs.1.stats_ref, f32[4,64,4096]{2,1,0:T(8,128)} %fisher_hbm.7, bf16[4,64,4096]{2,1,0:T(8,128)(2,1)} %params_hbm.7, s32[1]{0:T(128)S(4)} %get-tuple-element.22.after_ref), custom_call_target="tpu_custom_call" | custom-call | flops 15728640000 | bytes 1179648 | tf_op jit(solution)/shard_map/weigh_keep/pallas_call | solution.py:208
  23.1 0.3 collective-permute-done.7.two_ref
  23.4 0.2 split.3
  23.6 0.2 collective-permute-start.8
  23.9 2.9 %collective-permute-done.4.two_ref = bf16[16,7808]{1,0:T(8,128)(2,1)S(1)} collective-permute-done((bf16[16,7808]{1,0:T(8,128)(2,1)S(1)}, bf16[16,7808]{1,0:T(8,128)(2,1)S(1)}, u32[]{:S(2)}, u32[]{:S(2)}) %collective-permute-start.4) | collective-permute-done | bytes 249888 | tf_op jit(solution)/shard_map/ppermute | solution.py:26
  26.9 2.5 %collective-permute-start.5 = (bf16[16,2560]{1,0:T(8,128)(2,1)S(1)}, bf16[16,2560]{1,0:T(8,128)(2,1)S(1)}, u32[]{:S(2)}, u32[]{:S(2)}) collective-permute-start(bf16[16,2560]{1,0:T(8,128)(2,1)S(1)} %merge.2), channel_id=1, source_target_pairs={{0,16},{8,24},{16,0},{24,8},{1,17},{9,25},{17,1},{25,9},{2,18},{10... | collective-permute-start | bytes 245768 | tf_op jit(solution)/shard_map/ppermute | solution.py:26
  29.4 1.1 %collective-permute-done.8.two_ref = bf16[16,4736]{1,0:T(8,128)(2,1)S(1)} collective-permute-done((bf16[16,4736]{1,0:T(8,128)(2,1)S(1)}, bf16[16,4736]{1,0:T(8,128)(2,1)S(1)}, u32[]{:S(2)}, u32[]{:S(2)}) %collective-permute-start.8) | collective-permute-done | bytes 151584 | tf_op jit(solution)/shard_map/ppermute | solution.py:26
  30.6 2.0 %collective-permute-start.9 = (bf16[16,1536]{1,0:T(8,128)(2,1)S(1)}, bf16[16,1536]{1,0:T(8,128)(2,1)S(1)}, u32[]{:S(2)}, u32[]{:S(2)}) collective-permute-start(bf16[16,1536]{1,0:T(8,128)(2,1)S(1)} %merge.3), channel_id=1, source_target_pairs={{0,16},{8,24},{16,0},{24,8},{1,17},{9,25},{17,1},{25,9},{2,18},{10... | collective-permute-start | bytes 147464 | tf_op jit(solution)/shard_map/ppermute | solution.py:26
  32.7 2.0 %collective-permute-done.9 = bf16[16,1536]{1,0:T(8,128)(2,1)S(1)} collective-permute-done((bf16[16,1536]{1,0:T(8,128)(2,1)S(1)}, bf16[16,1536]{1,0:T(8,128)(2,1)S(1)}, u32[]{:S(2)}, u32[]{:S(2)}) %collective-permute-start.9) | collective-permute-done | bytes 49184 | tf_op jit(solution)/shard_map/ppermute | solution.py:26
  34.9 1.2 %collective-permute-done.10 = bf16[32,1536]{1,0:T(8,128)(2,1)S(1)} collective-permute-done((bf16[32,1536]{1,0:T(8,128)(2,1)S(1)}, bf16[32,1536]{1,0:T(8,128)(2,1)S(1)}, u32[]{:S(2)}, u32[]{:S(2)}) %collective-permute-start.10) | collective-permute-done | bytes 98336 | tf_op jit(solution)/shard_map/ppermute | solution.py:26
  36.2 0.8 %pad_maximum_fusion = bf16[64,4096]{1,0:T(8,128)(2,1)} fusion(bf16[64,1536]{1,0:T(8,128)(2,1)S(1)} %maximum_select_fusion.1, bf16[64,2560]{1,0:T(8,128)(2,1)S(1)} %maximum_select_fusion), kind=kLoop, calls=%fused_computation | loop fusion | flops 1048576 | bytes 1048576 | tf_op jit(solution)/shard_map/concatenate | solution.py:322
  (16 shorter events, 0.8 us)
Async XLA Ops:
  2.4 4.6 %collective-permute-start = (f32[8,128]{1,0:T(8,128)S(1)}, f32[8,128]{1,0:T(8,128)S(1)}, u32[]{:S(2)}, u32[]{:S(2)}) collective-permute-start(f32[8,128]{1,0:T(8,128)S(1)} %local_stats.1.one_ref), channel_id=1, source_target_pairs={{0,1},{1,0},{2,3},{3,2},{4,5},{5,4},{6,7},{7,6},{8,9},{9,8},{10,11... | collective-permute-start | bytes 12296 | tf_op jit(solution)/shard_map/ppermute | solution.py:26
  7.1 3.8 %collective-permute-start.1 = (f32[8,128]{1,0:T(8,128)S(1)}, f32[8,128]{1,0:T(8,128)S(1)}, u32[]{:S(2)}, u32[]{:S(2)}) collective-permute-start(f32[8,128]{1,0:T(8,128)S(1)} %get-tuple-element.15.one_ref), channel_id=1, source_target_pairs={{0,2},{1,3},{2,0},{3,1},{4,6},{5,7},{6,4},{7,5},{8,10},{9,11},{10,... | collective-permute-start | bytes 12296 | tf_op jit(solution)/shard_map/ppermute | solution.py:26
  10.9 4.7 %collective-permute-start.2 = (f32[8,128]{1,0:T(8,128)S(1)}, f32[8,128]{1,0:T(8,128)S(1)}, u32[]{:S(2)}, u32[]{:S(2)}) collective-permute-start(f32[8,128]{1,0:T(8,128)S(1)} %get-tuple-element.17), channel_id=1, source_target_pairs={{0,4},{1,5},{2,6},{3,7},{4,0},{5,1},{6,2},{7,3},{8,12},{9,13},{10,... | collective-permute-start | bytes 12296 | tf_op jit(solution)/shard_map/ppermute | solution.py:26
  15.9 2.2 %collective-permute-start.3 = (f32[2,32,2560]{2,1,0:T(8,128)S(1)}, f32[2,32,2560]{2,1,0:T(8,128)S(1)}, u32[]{:S(2)}, u32[]{:S(2)}) collective-permute-start(f32[2,32,2560]{2,1,0:T(8,128)S(1)} %weigh_fetched.1), channel_id=1, source_target_pairs={{0,8},{8,0},{16,24},{24,16},{1,9},{9,1},{17,25},{25,17},{2,10},{10... | collective-permute-start | bytes 1966088 | tf_op jit(solution)/shard_map/ppermute | solution.py:26
  18.4 8.4 %collective-permute-start.4 = (bf16[16,7808]{1,0:T(8,128)(2,1)S(1)}, bf16[16,7808]{1,0:T(8,128)(2,1)S(1)}, u32[]{:S(2)}, u32[]{:S(2)}) collective-permute-start(bf16[16,7808]{1,0:T(8,128)(2,1)S(1)} %get-tuple-element.21), channel_id=1, source_target_pairs={{0,16},{8,24},{16,0},{24,8},{1,17},{9,25},{17,1},{25,9},{2,18},{10... | collective-permute-start | bytes 749576 | tf_op jit(solution)/shard_map/ppermute | solution.py:26
  21.6 1.8 %collective-permute-start.7 = (f32[2,32,1536]{2,1,0:T(8,128)S(1)}, f32[2,32,1536]{2,1,0:T(8,128)S(1)}, u32[]{:S(2)}, u32[]{:S(2)}) collective-permute-start(f32[2,32,1536]{2,1,0:T(8,128)S(1)} %weigh_send.1), channel_id=1, source_target_pairs={{0,8},{8,0},{16,24},{24,16},{1,9},{9,1},{17,25},{25,17},{2,10},{10... | collective-permute-start | bytes 1179656 | tf_op jit(solution)/shard_map/ppermute | solution.py:26
  23.6 6.9 %collective-permute-start.8 = (bf16[16,4736]{1,0:T(8,128)(2,1)S(1)}, bf16[16,4736]{1,0:T(8,128)(2,1)S(1)}, u32[]{:S(2)}, u32[]{:S(2)}) collective-permute-start(bf16[16,4736]{1,0:T(8,128)(2,1)S(1)} %get-tuple-element.24), channel_id=1, source_target_pairs={{0,16},{8,24},{16,0},{24,8},{1,17},{9,25},{17,1},{25,9},{2,18},{10... | collective-permute-start | bytes 454664 | tf_op jit(solution)/shard_map/ppermute | solution.py:26
  26.9 5.7 %collective-permute-start.5 = (bf16[16,2560]{1,0:T(8,128)(2,1)S(1)}, bf16[16,2560]{1,0:T(8,128)(2,1)S(1)}, u32[]{:S(2)}, u32[]{:S(2)}) collective-permute-start(bf16[16,2560]{1,0:T(8,128)(2,1)S(1)} %merge.2), channel_id=1, source_target_pairs={{0,16},{8,24},{16,0},{24,8},{1,17},{9,25},{17,1},{25,9},{2,18},{10... | collective-permute-start | bytes 245768 | tf_op jit(solution)/shard_map/ppermute | solution.py:26
  30.6 4.2 %collective-permute-start.9 = (bf16[16,1536]{1,0:T(8,128)(2,1)S(1)}, bf16[16,1536]{1,0:T(8,128)(2,1)S(1)}, u32[]{:S(2)}, u32[]{:S(2)}) collective-permute-start(bf16[16,1536]{1,0:T(8,128)(2,1)S(1)} %merge.3), channel_id=1, source_target_pairs={{0,16},{8,24},{16,0},{24,8},{1,17},{9,25},{17,1},{25,9},{2,18},{10... | collective-permute-start | bytes 147464 | tf_op jit(solution)/shard_map/ppermute | solution.py:26
  32.6 2.2 %collective-permute-start.6 = (bf16[32,2560]{1,0:T(8,128)(2,1)S(1)}, bf16[32,2560]{1,0:T(8,128)(2,1)S(1)}, u32[]{:S(2)}, u32[]{:S(2)}) collective-permute-start(bf16[32,2560]{1,0:T(8,128)(2,1)S(1)} %maximum_select_fusion.2), channel_id=1, source_target_pairs={{0,8},{8,0},{16,24},{24,16},{1,9},{9,1},{17,25},{25,17},{2,10},{10... | collective-permute-start | bytes 491528 | tf_op jit(solution)/shard_map/ppermute | solution.py:26
  34.8 1.4 %collective-permute-start.10 = (bf16[32,1536]{1,0:T(8,128)(2,1)S(1)}, bf16[32,1536]{1,0:T(8,128)(2,1)S(1)}, u32[]{:S(2)}, u32[]{:S(2)}) collective-permute-start(bf16[32,1536]{1,0:T(8,128)(2,1)S(1)} %maximum_select_fusion.3), channel_id=1, source_target_pairs={{0,8},{8,0},{16,24},{24,16},{1,9},{9,1},{17,25},{25,17},{2,10},{10... | collective-permute-start | bytes 294920 | tf_op jit(solution)/shard_map/ppermute | solution.py:26
